TPU v7x, 32 devices: a whole 2x2x4 slice. The times are simulated.
32 devices in a mesh: chain: 8 (over z, core), dp: 4 (over y, x).
Axes of the slice: x: 2, y: 2, z: 4, core: 2. Of those that a mesh axis runs over, the one named last changes fastest.
Arguments:
- images_in: float32 [8, 1024, 1024], P('chain', 'dp'), may hold values from -8 to 8
- images_mid: float32 [8, 1024, 1024], P('chain', 'dp'), may hold values from -8 to 8
- images_out: float32 [8, 1024, 1000], P('chain', 'dp'), may hold values from -8 to 8
- ends_in: float32 [2, 1024, 1024], P(None, 'dp'), may hold values from -8 to 8
- ends_mid: float32 [2, 1024, 1024], P(None, 'dp'), may hold values from -8 to 8
- ends_out: float32 [2, 1024, 1000], P(None, 'dp'), may hold values from -8 to 8
- data_pool: bfloat16 [7168, 1024], P('dp'), may hold values from -6 to 6
- batch_rows: int32 [8, 3584], P('chain', 'dp'), may hold values from 0 to 1791
- labels: int32 [8, 3584], P('chain', 'dp'), may hold values from 0 to 999
- climbing: int32 [8], P('chain'), may hold values 0 or 1
Outputs:
- new_in: float32 [8, 1024, 1024], P('chain', 'dp')
- new_mid: float32 [8, 1024, 1024], P('chain', 'dp')
- new_out: float32 [8, 1024, 1000], P('chain', 'dp')
- energies: float32 [8], P('chain')
- arc_share: float32 [8], P('chain')
- bend: float32 [8], P('chain')
Inputs may be any that keep to these rules, and one draw needn't show every extreme that they name: batch_rows[i, b] names a row of the pool shard held by dp index b // 896.
All inputs are finite; a program needn't handle non-finite values. No bound on the sum of `climbing` on one device may be relied on, other than what follows from the above.
Results may differ from a plain program's by a relative error of at most 0.0023.
Values may be sent and summed in bfloat16 or wider, within the bound.
A program may use at most 128 MiB of HBM per device.

v0:
```python
import functools

import jax
import jax.numpy as jnp
from jax import lax
from jax.experimental import pallas as pl
from jax.experimental.pallas import tpu as pltpu
from jax.sharding import PartitionSpec as P

SPRING = 0.03
EPS = 1e-06
TILE = 256
LANES = 128
F32 = jnp.float32
BF16 = jnp.bfloat16


def copies_of(count, chain, chunks):
    pairs = count // 2
    gather = 1 + (pairs - 1) + pairs
    scatter = pairs
    return (2 + chunks) * (gather + scatter + pairs) + 3 + 2 * (count - 1) + (chain - 1) + 9


def dot_nn(left, right):
    return jnp.dot(left, right, preferred_element_type=F32)


def dot_nt(left, right):
    return lax.dot_general(left, right, (((1,), (1,)), ((), ())), preferred_element_type=F32)


def dot_tn(left, right):
    return lax.dot_general(left, right, (((0,), (0,)), ((), ())), preferred_element_type=F32)


def fold(value):
    part = jnp.sum(value.reshape(value.shape[0] // 8, 8, value.shape[1]), axis=0)
    total = part[:, :LANES]
    for k in range(1, value.shape[1] // LANES):
        total = total + part[:, k * LANES : (k + 1) * LANES]
    return total


def whole(tile):
    return jnp.sum(tile, axis=(0, 1), keepdims=True)


def kernel(
    n,
    c,
    classes,
    p_in,
    p_mid,
    p_out,
    e_in,
    e_mid,
    e_out,
    pool,
    picks,
    labs,
    climb,
    o_in,
    o_mid,
    o_out,
    o_energy,
    o_arc,
    o_bend,
    own,
    edge,
    thin,
    tau,
    wide,
    stage,
    near,
    before,
    after,
    pool_v,
    hot,
    lab_t,
    lab_out,
    lab_in,
    rows_out,
    rows,
    slope,
    hid,
    resid,
    rows_t,
    hid_t,
    resid_t,
    dlog,
    dres,
    grad,
    from_core,
    from_pair,
    last,
    power,
    sums,
    spans,
    late,
    load_sem,
    send_sem,
    recv_sem,
):
    ci, me = lax.axis_index("chain"), lax.axis_index("dp")
    pairs = n // 2
    core, side = lax.rem(ci, 2), lax.rem(me, 2)
    pair = me // 2
    leads = core == side
    moves = core != side
    cross = (ci + 1 - 2 * core, me + 1 - 2 * side)
    twin = (ci + 1 - 2 * core, me)
    block, width = own.shape[1], own.shape[2]
    depth = n * block
    step = min(32, block)
    batch = rows.shape[0]
    tiles = width // TILE
    factor = (depth**-0.5, width**-0.5, depth**-0.5)
    norm = 1.0 / (batch * n * classes)
    counter = [0]

    def remote(src, dst, to):
        k = counter[0]
        counter[0] += 1
        copy = pltpu.make_async_remote_copy(
            src_ref=src,
            dst_ref=dst,
            send_sem=send_sem.at[k],
            recv_sem=recv_sem.at[k],
            device_id=to,
            device_id_type=pl.DeviceIdType.MESH,
        )
        return copy

    def pair_at(d):
        return lax.rem(pair + d, pairs)

    barrier = pltpu.get_barrier_semaphore()
    for d in range(1, n):
        pl.semaphore_signal(
            barrier, inc=1, device_id=(ci, lax.rem(me + d, n)), device_id_type=pl.DeviceIdType.MESH
        )
    for d in range(1, c):
        pl.semaphore_signal(
            barrier, inc=1, device_id=(lax.rem(ci + d, c), me), device_id_type=pl.DeviceIdType.MESH
        )

    pl.semaphore_signal(barrier, inc=1, device_id=cross, device_id_type=pl.DeviceIdType.MESH)

    end = jnp.where(ci == 0, 0, 1)
    loads = [
        pltpu.make_async_copy(p_in.at[0], own.at[0], load_sem.at[0]),
        pltpu.make_async_copy(p_mid.at[0], own.at[1], load_sem.at[1]),
        pltpu.make_async_copy(p_out.at[0], thin.at[0, pl.ds(0, classes)], load_sem.at[2]),
        pltpu.make_async_copy(pool, pool_v, load_sem.at[3]),
        pltpu.make_async_copy(e_in.at[end], edge.at[0], load_sem.at[4]),
        pltpu.make_async_copy(e_mid.at[end], edge.at[1], load_sem.at[5]),
        pltpu.make_async_copy(e_out.at[end], thin.at[1, pl.ds(0, classes)], load_sem.at[6]),
    ]
    for load in loads:
        load.start()

    def turned(into, thin_at):
        @pl.loop(0, width // LANES)
        def _(k):
            at = pl.ds(pl.multiple_of(k * LANES, LANES), LANES)
            into[:, at] = thin[thin_at, at, :].T

    def blanked(thin_at):
        if classes < width:
            thin[thin_at, pl.ds(classes, width - classes), :] = jnp.zeros(
                (width - classes, block), F32
            )

    def lowered(m):
        def body(r, _):
            off = pl.multiple_of(r * step, step)
            value = own[m, pl.ds(off, step), :]
            low = (value * factor[m]).astype(BF16)
            stage[m, pl.ds(off, step), :] = low

            @pl.when(leads)
            def _():
                wide[m, pl.ds(pl.multiple_of(me * block + off, step), step), :] = low

            near[m, pl.ds(off, step), :] = value.astype(BF16)
            return 0

        lax.fori_loop(0, block // step, body, 0)

    for m in range(2):
        loads[m].wait()
        lowered(m)
    blanked(0)
    blanked(1)
    pl.semaphore_wait(barrier, n - 1 + c - 1 + 1)

    def column(t):
        return pl.ds(pl.multiple_of(t * TILE, TILE), TILE)

    everything = pl.ds(0, width)

    def piece(ref, m, index, at=everything):
        return ref.at[m, pl.ds(pl.multiple_of(index * block, block), block), at]

    started = []

    def begin(copy):
        copy.start()
        started.append(copy)
        return copy

    hop, across, over = {}, {}, {}

    def swap(src, dst):
        copy = remote(src, dst, cross)

        @pl.when(moves)
        def _():
            copy.start()

        swapped.append(copy)
        return copy

    def arrive(copy):
        @pl.when(moves)
        def _():
            copy.wait_recv()

    swapped = []

    def send_own(key, m, at=everything):
        hop[key] = swap(stage.at[m, :, at], piece(wide, m, me, at))

    def spread(key, m, at=everything):
        arrive(hop[key])
        held = piece(wide, m, 2 * pair + core, at)
        across[key] = [
            begin(remote(held, held, (ci, 2 * pair_at(d) + side))) for d in range(1, pairs)
        ]
        over[key] = [begin(remote(held, held, twin))]

    def forward(key, m, at=everything):
        for d in range(1, pairs):
            across[key][d - 1].wait_recv()
            held = piece(wide, m, 2 * pair_at(pairs - d) + core, at)
            over[key].append(begin(remote(held, held, twin)))

    def gathered(key):
        for copy in over[key]:
            copy.wait_recv()

    def chunk(step_of, t):
        step_of((2, t), 2, pl.ds(t * TILE, TILE))

    send_own(0, 0)

    lab_rows = jnp.broadcast_to(labs[...], (8, batch))
    lab_out[...] = lab_rows

    @pl.when(leads)
    def _():
        lab_in[...] = lab_rows

    row_of = jnp.broadcast_to(picks[...], (LANES, batch)).T
    lane = lax.broadcasted_iota(jnp.int32, (batch, LANES), 1)
    for k in range(pool_v.shape[0] // LANES):
        hot[:, k * LANES : (k + 1) * LANES] = (row_of == lane + k * LANES).astype(F32).astype(BF16)
    loads[3].wait()

    @pl.loop(0, tiles)
    def _(t):
        at = column(t)
        picked = dot_nn(hot[...], pool_v[:, at]).astype(BF16)
        rows_out[:, at] = picked

        @pl.when(leads)
        def _():
            rows[:, at] = picked

    lab_swap = swap(lab_out, lab_in)
    row_swap = swap(rows_out, rows)
    send_own(1, 1)
    loads[2].wait()
    turned(own.at[2], 0)
    lowered(2)
    spread(0, 0)
    for t in range(tiles):
        chunk(send_own, t)
    ups = [remote(near.at[m], before.at[m], (lax.rem(ci + 1, c), me)) for m in range(3)]
    downs = [remote(near.at[m], after.at[m], (lax.rem(ci + c - 1, c), me)) for m in range(3)]
    has_next, has_prev = ci < c - 1, ci > 0

    @pl.when(has_next)
    def _():
        for copy in ups:
            copy.start()

    @pl.when(has_prev)
    def _():
        for copy in downs:
            copy.start()

    forward(0, 0)
    for load in loads[4:]:
        load.wait()
    turned(edge.at[2], 1)

    @pl.when(has_prev)
    def _():
        for copy in ups:
            copy.wait_recv()

    @pl.when(has_next)
    def _():
        for copy in downs:
            copy.wait_recv()

    def differences(m, at):
        mine = own[m, at, :]
        fixed = edge[m, at, :]
        left = jnp.where(ci == 0, fixed, before[m, at, :].astype(F32))
        right = jnp.where(ci == c - 1, fixed, after[m, at, :].astype(F32))
        return right - mine, mine - left

    zero = jnp.zeros((8, LANES), F32)

    def span_sums(m, carry):
        def body(r, carry):
            ahead, behind = differences(m, pl.ds(pl.multiple_of(r * step, step), step))
            return (
                carry[0] + fold(ahead * ahead),
                carry[1] + fold(behind * behind),
                carry[2] + fold(ahead * behind),
            )

        return lax.fori_loop(0, block // step, body, carry)

    carry = (zero, zero, zero)
    for m in range(3):
        carry = span_sums(m, carry)
    for k in range(3):
        sums[me, k] = carry[k]
    sums_out = [
        begin(remote(sums.at[me], sums.at[me], (ci, lax.rem(me + d, n)))) for d in range(1, n)
    ]

    arrive(lab_swap)
    lab_t[...] = jnp.broadcast_to(lab_in[...][0:1, :], (LANES, batch)).T
    arrive(row_swap)

    @pl.loop(0, tiles)
    def _(t):
        at = column(t)
        rows_t[at, :] = rows[:, at].T

    gathered(0)

    @pl.loop(0, tiles)
    def _(t):
        at = column(t)
        pre = dot_nn(rows[...], wide[0, :, at])
        sig = jax.nn.sigmoid(pre)
        value = (pre * sig).astype(BF16)
        hid[:, at] = value
        hid_t[at, :] = value.T
        slope[:, at] = sig * (1.0 + pre * (1.0 - sig))

    spread(1, 1)
    chunk(spread, 0)
    forward(1, 1)
    for t in range(1, tiles):
        chunk(spread, t)

    for copy in sums_out:
        copy.wait_recv()

    def over_dp(ref, k):
        total = ref[0, k]
        for j in range(1, n):
            total = total + ref[j, k]
        return whole(total)

    sq_ahead, sq_behind, mixed = (over_dp(sums, k) for k in range(3))
    len_ahead = jnp.sqrt(sq_ahead + EPS)
    len_behind = jnp.sqrt(sq_behind + EPS)
    raw_sq = (
        sq_ahead / (len_ahead * len_ahead)
        + sq_behind / (len_behind * len_behind)
        + 2.0 * mixed / (len_ahead * len_behind)
    )
    raw_len = jnp.sqrt(raw_sq + EPS)
    spans[ci, 0] = jnp.broadcast_to(len_behind, (8, LANES))
    spans[ci, 1] = jnp.broadcast_to(len_ahead, (8, LANES))
    spans_out = [
        begin(remote(spans.at[ci], spans.at[ci], (lax.rem(ci + d, c), me))) for d in range(1, c)
    ]

    gathered(1)

    @pl.loop(0, tiles)
    def _(t):
        at = column(t)
        value = (rows[:, at].astype(F32) + dot_nn(hid[...], wide[1, :, at])).astype(BF16)
        resid[:, at] = value
        resid_t[at, :] = value.T

    chunk(forward, 0)

    def classify(t, energy):
        at = column(t)
        logits = dot_nn(resid[...], wide[2, :, at])
        parts = []
        for k in range(TILE // LANES):
            target = (lab_t[...] == lane + (t * TILE + k * LANES)).astype(F32)
            err = logits[:, k * LANES : (k + 1) * LANES] - target
            energy = energy + fold(err * err)
            parts.append((err * norm).astype(BF16))
        dlog[:, at] = jnp.concatenate(parts, axis=1)
        return energy

    def products(m, left_t, right):
        @pl.loop(0, depth // TILE)
        def _(t):
            at = column(t)
            grad[m, at, :] = dot_nn(left_t[at, :], right[...]).astype(BF16)

    to_core, to_pair, to_home = {}, {}, {}

    def scatter(key, m, at=everything):
        to_core[key] = [
            begin(remote(piece(grad, m, 2 * q + 1 - core, at), from_core.at[m, q, :, at], twin))
            for q in range(pairs)
        ]

    def combine(m, into, index, parts, cols=everything):
        @pl.loop(0, block // step)
        def _(r):
            off = pl.multiple_of(r * step, step)
            at = pl.ds(pl.multiple_of(index * block + off, step), step)
            total = grad[m, at, cols].astype(F32)
            for part in parts:
                total = total + part[pl.ds(off, step), :].astype(F32)
            into[pl.ds(off, step), :] = total.astype(BF16)

    def scatter_on(key, m, at=everything):
        for copy in to_core[key]:
            copy.wait_recv()
        to_pair.setdefault(m, [])
        for d in range(1, pairs):
            q = pair_at(d)
            held = piece(grad, m, 2 * q + core, at)
            combine(m, held, 2 * q + core, [from_core.at[m, q, :, at]], at)
            to_pair[m].append(
                begin(remote(held, from_pair.at[m, d - 1, :, at], (ci, 2 * q + side)))
            )

    def scatter_home(m):
        for copy in to_pair[m]:
            copy.wait_recv()
        parts = [from_core.at[m, pair]] + [from_pair.at[m, d] for d in range(pairs - 1)]
        held = piece(grad, m, 2 * pair + core)
        combine(m, held, 2 * pair + core, parts)

        @pl.when(leads)
        def _():
            @pl.loop(0, block // step)
            def _(r):
                off = pl.multiple_of(r * step, step)
                at = pl.ds(pl.multiple_of(me * block + off, step), step)
                last[m, pl.ds(off, step), :] = grad[m, at, :]

        to_home[m] = swap(held, last.at[m])

    energy = zero
    for t in range(tiles):
        if t + 1 < tiles:
            chunk(forward, t + 1)
        gathered((2, t))
        energy = classify(t, energy)
        at = pl.ds(t * TILE, TILE)

        @pl.loop(0, depth // TILE)
        def _(r):
            of = column(r)
            grad[2, of, at] = dot_nn(resid_t[of, :], dlog[:, at]).astype(BF16)

        scatter((2, t), 2, at)
        if t > 0:
            chunk(scatter_on, t - 1)

    @pl.loop(0, depth // TILE)
    def _(t):
        at = column(t)
        dres[:, at] = dot_nt(dlog[...], wide[2, at, :]).astype(BF16)

    chunk(scatter_on, tiles - 1)

    products(1, hid_t, dres)
    scatter(1, 1)

    @pl.loop(0, depth // TILE)
    def _(t):
        at = column(t)
        dlog[:, at] = (dot_nt(dres[...], wide[1, at, :]) * slope[:, at]).astype(BF16)

    scatter_on(1, 1)
    products(0, rows_t, dlog)
    scatter(0, 0)
    power[0] = energy * (0.5 * norm)
    power_swap = swap(power.at[0], power.at[1])

    scatter_on(0, 0)
    scatter_home(2)

    for copy in spans_out:
        copy.wait_recv()
    by_ahead = 1.0 / (len_ahead * raw_len)
    by_behind = 1.0 / (len_behind * raw_len)

    for m in range(3):

        def body(r, _, m=m):
            at = pl.ds(pl.multiple_of(r * step, step), step)
            ahead, behind = differences(m, at)
            tau[m, at, :] = ahead * by_ahead + behind * by_behind
            return 0

        lax.fori_loop(0, block // step, body, 0)

    arc = jnp.zeros((1, 1), F32)
    band = jnp.zeros((1, 1), F32)
    for k in range(c):
        length = spans[k, 0, 0:1, 0:1]
        arc = arc + jnp.where(k <= ci, length, 0.0)
        band = band + length
    band = band + spans[c - 1, 1, 0:1, 0:1]

    for m in (1, 0):
        scatter_home(m)
    arrive(power_swap)

    def finish(m, carry):
        arrive(to_home[m])

        def body(r, carry):
            at = pl.ds(pl.multiple_of(r * step, step), step)
            total = last[m, at, :].astype(F32) * factor[m]
            edge[m, at, :] = total
            return carry[0] + fold(total * tau[m, at, :]), carry[1] + fold(total * total)

        return lax.fori_loop(0, block // step, body, carry)

    carry = (zero, zero)
    for m in (2, 1, 0):
        carry = finish(m, carry)
    late[me, 0] = carry[0]
    late[me, 1] = carry[1]
    late[me, 2] = jnp.where(leads, power[0], power[1])
    late_out = [
        begin(remote(late.at[me], late.at[me], (ci, lax.rem(me + d, n)))) for d in range(1, n)
    ]
    for copy in late_out:
        copy.wait_recv()
    along, g_g, energy_all = (over_dp(late, k) for k in range(3))

    goal = (ci + 1).astype(F32) / (c + 1) * band
    coef = jnp.where(jnp.full((1, 1), climb[0]) == 1, 2.0 * along, along + SPRING * (goal - arc) / band)
    tau_sq = raw_sq / (raw_sq + EPS)
    force_sq = g_g - 2.0 * coef * along + coef * coef * tau_sq
    scale = band / (c + 1) / jnp.sqrt(force_sq + EPS)
    push = scale * coef
    o_energy[0] = energy_all[0, 0]
    o_arc[0] = (arc / band)[0, 0]
    o_bend[0] = (0.5 * raw_len)[0, 0]

    stores = []
    for m, out in ((2, o_out), (1, o_mid), (0, o_in)):
        if m == 2:

            @pl.loop(0, width // LANES)
            def _(k):
                at = pl.ds(pl.multiple_of(k * LANES, LANES), LANES)
                new = own[2, :, at] + (push * tau[2, :, at] - scale * edge[2, :, at])
                thin[0, at, :] = new.T

            source = thin.at[0, pl.ds(0, classes)]
        else:

            @pl.loop(0, block // step)
            def _(r):
                at = pl.ds(pl.multiple_of(r * step, step), step)
                tau[m, at, :] = own[m, at, :] + (push * tau[m, at, :] - scale * edge[m, at, :])

            source = tau.at[m]
        copy = pltpu.make_async_copy(source, out.at[0], load_sem.at[m])
        copy.start()
        stores.append(copy)

    @pl.when(has_next)
    def _():
        for copy in ups:
            copy.wait_send()

    @pl.when(has_prev)
    def _():
        for copy in downs:
            copy.wait_send()

    @pl.when(moves)
    def _():
        for copy in swapped:
            copy.wait_send()

    for copy in started:
        copy.wait_send()
    for copy in stores:
        copy.wait()


def on_device(
    n,
    c,
    images_in,
    images_mid,
    images_out,
    ends_in,
    ends_mid,
    ends_out,
    data_pool,
    batch_rows,
    labels,
    climbing,
):
    block, width = images_in.shape[1], images_in.shape[2]
    classes = images_out.shape[2]
    depth = n * block
    batch = batch_rows.shape[1]
    pairs = n // 2
    copies = copies_of(n, c, width // TILE)
    vmem = pl.BlockSpec(memory_space=pltpu.VMEM)
    anywhere = pl.BlockSpec(memory_space=pl.ANY)
    scalar = pl.BlockSpec(memory_space=pltpu.SMEM)
    small = jax.ShapeDtypeStruct((1,), F32)
    outs = pl.pallas_call(
        functools.partial(kernel, n, c, classes),
        out_shape=(
            jax.ShapeDtypeStruct(images_in.shape, F32),
            jax.ShapeDtypeStruct(images_mid.shape, F32),
            jax.ShapeDtypeStruct((1, classes, block), F32),
            small,
            small,
            small,
        ),
        in_specs=[anywhere] * 7 + [vmem] * 2 + [scalar],
        out_specs=[anywhere] * 3 + [scalar] * 3,
        scratch_shapes=[
            pltpu.VMEM((3, block, width), F32),
            pltpu.VMEM((3, block, width), F32),
            pltpu.VMEM((2, width, block), F32),
            pltpu.VMEM((3, block, width), F32),
            pltpu.VMEM((3, depth, width), BF16),
            pltpu.VMEM((3, block, width), BF16),
            pltpu.VMEM((3, block, width), BF16),
            pltpu.VMEM((3, block, width), BF16),
            pltpu.VMEM((3, block, width), BF16),
            pltpu.VMEM(data_pool.shape, BF16),
            pltpu.VMEM((batch, data_pool.shape[0]), BF16),
            pltpu.VMEM((batch, LANES), jnp.int32),
            pltpu.VMEM((8, batch), jnp.int32),
            pltpu.VMEM((8, batch), jnp.int32),
            pltpu.VMEM((batch, depth), BF16),
            pltpu.VMEM((batch, depth), BF16),
            pltpu.VMEM((batch, width), F32),
            pltpu.VMEM((batch, width), BF16),
            pltpu.VMEM((batch, depth), BF16),
            pltpu.VMEM((depth, batch), BF16),
            pltpu.VMEM((width, batch), BF16),
            pltpu.VMEM((depth, batch), BF16),
            pltpu.VMEM((batch, width), BF16),
            pltpu.VMEM((batch, depth), BF16),
            pltpu.VMEM((3, depth, width), BF16),
            pltpu.VMEM((3, pairs, block, width), BF16),
            pltpu.VMEM((3, max(pairs - 1, 1), block, width), BF16),
            pltpu.VMEM((3, block, width), BF16),
            pltpu.VMEM((2, 8, LANES), F32),
            pltpu.VMEM((n, 3, 8, LANES), F32),
            pltpu.VMEM((c, 2, 8, LANES), F32),
            pltpu.VMEM((n, 3, 8, LANES), F32),
            pltpu.SemaphoreType.DMA((7,)),
            pltpu.SemaphoreType.DMA((copies,)),
            pltpu.SemaphoreType.DMA((copies,)),
        ],
        compiler_params=pltpu.CompilerParams(
            collective_id=0, has_side_effects=True, vmem_limit_bytes=63 * 1024 * 1024
        ),
    )(
        images_in,
        images_mid,
        jnp.swapaxes(images_out, 1, 2),
        ends_in,
        ends_mid,
        jnp.swapaxes(ends_out, 1, 2),
        data_pool,
        batch_rows,
        labels,
        climbing,
    )
    return (outs[0], outs[1], jnp.swapaxes(outs[2], 1, 2), *outs[3:])


def solution(mesh):
    placed = (
        P("chain", "dp", None),
        P("chain", "dp", None),
        P("chain", "dp", None),
        P(None, "dp", None),
        P(None, "dp", None),
        P(None, "dp", None),
        P("dp", None),
        P("chain", "dp"),
        P("chain", "dp"),
        P("chain"),
    )
    return jax.shard_map(
        functools.partial(on_device, mesh.shape["dp"], mesh.shape["chain"]),
        mesh=mesh,
        in_specs=placed,
        out_specs=(
            P("chain", "dp", None),
            P("chain", "dp", None),
            P("chain", "dp", None),
            P("chain"),
            P("chain"),
            P("chain"),
        ),
        check_vma=False,
    )
```

profile of v0, /device:TPU:0, one launch (start us, length us, event | category | flops | bytes accessed | tf_op | source)
XLA Modules:
  0.0 125.3 jit_solution(4062360949744338251)
XLA Ops:
  1.3 114.4 %shard_map.145 = (f32[1,256,1024]{2,1,0:T(8,128)}, f32[1,256,1024]{2,1,0:T(8,128)}, f32[1,1000,256]{2,1,0:T(8,128)}, f32[1]{0:T(128)}, f32[1]{0:T(128)}, /*index=5*/f32[1]{0:T(128)}) custom-call(f32[1,256,1024]{2,1,0:T(8,128)} %p_in.1, f32[1,256,1024]{2,1,0:T(8,128)} %p_mid.1, f32[1,1000,256]{2,1,0:T(8,128)} %bitcast.4, f32[2,256,1024]{2,1,0:T(8,128)} %e_in.1, ...), custom_call_target="tpu_custom_call" | custom-call | tf_op jit(solution)/shard_map/pallas_call | solution.py:645
  115.7 0.0 copy-start
  115.7 0.0 copy-start.1
  115.7 2.5 %copy.23 = f32[1,256,1024]{2,1,0:T(8,128)} copy(f32[1,256,1024]{2,1,0:T(8,128)} %get-tuple-element.24) | data formatting | bytes 2097152
  118.2 0.0 copy-done
  118.2 1.0 copy.24
  119.1 0.0 copy-done.1
  119.1 1.0 copy.25
Async XLA Ops:
  115.7 2.5 %copy-start = (f32[1,256,1024]{2,1,0:T(8,128)S(1)}, f32[1,256,1024]{2,1,0:T(8,128)}, u32[]{:S(2)}) copy-start(f32[1,256,1024]{2,1,0:T(8,128)} %get-tuple-element.25) | copy-start | bytes 3145732
  115.7 3.4 %copy-start.1 = (f32[1,1000,256]{2,1,0:T(8,128)S(1)}, f32[1,1000,256]{2,1,0:T(8,128)}, u32[]{:S(2)}) copy-start(f32[1,1000,256]{2,1,0:T(8,128)} %get-tuple-element.14) | copy-start | bytes 3072004
where the time goes:
time: 127 us; the launch traced here: 125 us
  Pallas kernels  114 us (90%)
  between operations  6.5 us (5%)
  local copies, waits for them, and re-layouts  4.39 us (3%)
    pallas_call x1, Pallas kernels, on_device(): pl.pallas_call(functools.partial(kernel, n, c, classes), out_shape=(jax.S...  114 us
    unnamed x7, local copies, waits for them, and re-layouts  4.39 us

commit v1 on v0

--- a/solution.py
+++ b/solution.py
@@ -17,9 +17,9 @@
 
 def copies_of(count, chain, chunks):
     pairs = count // 2
-    gather = 1 + (pairs - 1) + pairs
-    scatter = pairs
-    return (2 + chunks) * (gather + scatter + pairs) + 3 + 2 * (count - 1) + (chain - 1) + 9
+    gather = (2 + chunks) * (1 + (pairs - 1) + pairs)
+    scatter = 3 * chunks * (pairs + (pairs - 1) + 1)
+    return gather + scatter + 6 + 2 * (count - 1) + (chain - 1) + 2 + 2
 
 
 def dot_nn(left, right):
@@ -188,17 +188,12 @@
 
         lax.fori_loop(0, block // step, body, 0)
 
-    for m in range(2):
-        loads[m].wait()
-        lowered(m)
-    blanked(0)
-    blanked(1)
-    pl.semaphore_wait(barrier, n - 1 + c - 1 + 1)
-
     def column(t):
         return pl.ds(pl.multiple_of(t * TILE, TILE), TILE)
 
     everything = pl.ds(0, width)
+    tail = TILE if batch > TILE else 0
+    blocks = [pl.ds(0, batch - tail)] + ([pl.ds(batch - tail, tail)] if tail else [])
 
     def piece(ref, m, index, at=everything):
         return ref.at[m, pl.ds(pl.multiple_of(index * block, block), block), at]
@@ -211,34 +206,50 @@
         return copy
 
     hop, across, over = {}, {}, {}
+    swapped = []
 
     def swap(src, dst):
         copy = remote(src, dst, cross)
-
+        swapped.append(copy)
+        return copy
+
+    def send(*copies):
         @pl.when(moves)
         def _():
-            copy.start()
-
-        swapped.append(copy)
-        return copy
-
-    def arrive(copy):
+            for copy in copies:
+                copy.start()
+
+    def arrive(*copies):
         @pl.when(moves)
         def _():
-            copy.wait_recv()
-
-    swapped = []
-
-    def send_own(key, m, at=everything):
+            for copy in copies:
+                copy.wait_recv()
+
+    def prepare(key, m, at=everything):
         hop[key] = swap(stage.at[m, :, at], piece(wide, m, me, at))
-
-    def spread(key, m, at=everything):
-        arrive(hop[key])
         held = piece(wide, m, 2 * pair + core, at)
         across[key] = [
-            begin(remote(held, held, (ci, 2 * pair_at(d) + side))) for d in range(1, pairs)
+            remote(held, held, (ci, 2 * pair_at(d) + side)) for d in range(1, pairs)
         ]
-        over[key] = [begin(remote(held, held, twin))]
+        over[key] = [remote(held, held, twin)]
+        started.extend(across[key] + over[key])
+
+    def spread(key):
+        for copy in across[key] + over[key][:1]:
+            copy.start()
+
+    def spread_own(*keys):
+        @pl.when(leads)
+        def _():
+            for key in keys:
+                spread(key)
+
+    def spread_moved(*keys):
+        @pl.when(moves)
+        def _():
+            for key in keys:
+                hop[key].wait_recv()
+                spread(key)
 
     def forward(key, m, at=everything):
         for d in range(1, pairs):
@@ -250,10 +261,44 @@
         for copy in over[key]:
             copy.wait_recv()
 
-    def chunk(step_of, t):
-        step_of((2, t), 2, pl.ds(t * TILE, TILE))
-
-    send_own(0, 0)
+    def cols(t):
+        return pl.ds(t * TILE, TILE)
+
+    parts = [(2, t) for t in range(tiles)]
+    for m in range(2):
+        prepare(m, m)
+    for key in parts:
+        prepare(key, 2, cols(key[1]))
+
+    loads[0].wait()
+    lowered(0)
+    pl.semaphore_wait(barrier, n - 1 + c - 1 + 1)
+    send(hop[0])
+    spread_own(0)
+    loads[1].wait()
+    lowered(1)
+    send(hop[1])
+    spread_own(1)
+    blanked(0)
+    blanked(1)
+    loads[2].wait()
+    turned(own.at[2], 0)
+    lowered(2)
+    spread_own(*parts)
+
+    ups = [remote(near.at[m], before.at[m], (lax.rem(ci + 1, c), me)) for m in range(3)]
+    downs = [remote(near.at[m], after.at[m], (lax.rem(ci + c - 1, c), me)) for m in range(3)]
+    has_next, has_prev = ci < c - 1, ci > 0
+
+    @pl.when(has_next)
+    def _():
+        for copy in ups:
+            copy.start()
+
+    @pl.when(has_prev)
+    def _():
+        for copy in downs:
+            copy.start()
 
     lab_rows = jnp.broadcast_to(labs[...], (8, batch))
     lab_out[...] = lab_rows
@@ -262,45 +307,33 @@
     def _():
         lab_in[...] = lab_rows
 
+    lab_swap = swap(lab_out, lab_in)
+    send(lab_swap)
     row_of = jnp.broadcast_to(picks[...], (LANES, batch)).T
     lane = lax.broadcasted_iota(jnp.int32, (batch, LANES), 1)
     for k in range(pool_v.shape[0] // LANES):
         hot[:, k * LANES : (k + 1) * LANES] = (row_of == lane + k * LANES).astype(F32).astype(BF16)
     loads[3].wait()
-
-    @pl.loop(0, tiles)
-    def _(t):
-        at = column(t)
-        picked = dot_nn(hot[...], pool_v[:, at]).astype(BF16)
-        rows_out[:, at] = picked
-
-        @pl.when(leads)
-        def _():
-            rows[:, at] = picked
-
-    lab_swap = swap(lab_out, lab_in)
-    row_swap = swap(rows_out, rows)
-    send_own(1, 1)
-    loads[2].wait()
-    turned(own.at[2], 0)
-    lowered(2)
-    spread(0, 0)
-    for t in range(tiles):
-        chunk(send_own, t)
-    ups = [remote(near.at[m], before.at[m], (lax.rem(ci + 1, c), me)) for m in range(3)]
-    downs = [remote(near.at[m], after.at[m], (lax.rem(ci + c - 1, c), me)) for m in range(3)]
-    has_next, has_prev = ci < c - 1, ci > 0
-
-    @pl.when(has_next)
-    def _():
-        for copy in ups:
-            copy.start()
-
-    @pl.when(has_prev)
-    def _():
-        for copy in downs:
-            copy.start()
-
+    row_swap = []
+    for b, rs in enumerate(blocks):
+
+        @pl.loop(0, tiles)
+        def _(t):
+            at = column(t)
+            picked = dot_nn(hot[rs, :], pool_v[:, at]).astype(BF16)
+            rows_out[rs, at] = picked
+
+            @pl.when(leads)
+            def _():
+                rows[rs, at] = picked
+
+        row_swap.append(swap(rows_out.at[rs], rows.at[rs]))
+        send(row_swap[b])
+        if b == 0:
+            send(hop[parts[0]])
+    send(*[hop[key] for key in parts[1:]])
+
+    spread_moved(0, 1)
     forward(0, 0)
     for load in loads[4:]:
         load.wait()
@@ -345,32 +378,164 @@
         begin(remote(sums.at[me], sums.at[me], (ci, lax.rem(me + d, n)))) for d in range(1, n)
     ]
 
+    gathered(0)
     arrive(lab_swap)
     lab_t[...] = jnp.broadcast_to(lab_in[...][0:1, :], (LANES, batch)).T
-    arrive(row_swap)
+
+    def activate(rs):
+        @pl.loop(0, tiles)
+        def _(t):
+            at = column(t)
+            pre = dot_nn(rows[rs, :], wide[0, :, at])
+            sig = jax.nn.sigmoid(pre)
+            value = (pre * sig).astype(BF16)
+            hid[rs, at] = value
+            hid_t[at, rs] = value.T
+            slope[rs, at] = sig * (1.0 + pre * (1.0 - sig))
+
+    def residual(rs):
+        @pl.loop(0, tiles)
+        def _(t):
+            at = column(t)
+            value = (rows[rs, at].astype(F32) + dot_nn(hid[rs, :], wide[1, :, at])).astype(BF16)
+            resid[rs, at] = value
+            resid_t[at, rs] = value.T
+
+    for b, rs in enumerate(blocks):
+        arrive(row_swap[b])
+        activate(rs)
+        if b == 0:
+            spread_moved(parts[0])
+            forward(1, 1)
+            gathered(1)
+        residual(rs)
+
+    if tiles > 1:
+        spread_moved(parts[1])
+    forward(parts[0], 2, cols(0))
+
+    def classify(t, energy):
+        at = column(t)
+        logits = dot_nn(resid[...], wide[2, :, at])
+        out = []
+        for k in range(TILE // LANES):
+            target = (lab_t[...] == lane + (t * TILE + k * LANES)).astype(F32)
+            err = logits[:, k * LANES : (k + 1) * LANES] - target
+            energy = energy + fold(err * err)
+            out.append((err * norm).astype(BF16))
+        dlog[:, at] = jnp.concatenate(out, axis=1)
+        return energy
+
+    def product(m, left_t, right, at):
+        half = depth // 2
+
+        @pl.loop(0, 2)
+        def _(r):
+            of = pl.ds(pl.multiple_of(r * half, half), half)
+            grad[m, of, at] = dot_nn(left_t[of, :], right[:, at]).astype(BF16)
+
+    to_core, to_pair, to_home = {}, {}, {}
+
+    def scatter(key, m, at):
+        to_core[key] = [
+            begin(remote(piece(grad, m, 2 * q + 1 - core, at), from_core.at[m, q, :, at], twin))
+            for q in range(pairs)
+        ]
+        to_pair[key] = []
+        for d in range(1, pairs):
+            q = pair_at(d)
+            held = piece(grad, m, 2 * q + core, at)
+            to_pair[key].append(remote(held, from_pair.at[m, d - 1, :, at], (ci, 2 * q + side)))
+        started.extend(to_pair[key])
+        held = piece(grad, m, 2 * pair + core, at)
+        to_home[key] = swap(held, last.at[m, :, at])
+
+    def combine(m, into, index, terms, at):
+        @pl.loop(0, block // step)
+        def _(r):
+            off = pl.multiple_of(r * step, step)
+            of = pl.ds(pl.multiple_of(index * block + off, step), step)
+            total = grad[m, of, at].astype(F32)
+            for term in terms:
+                total = total + term[pl.ds(off, step), :].astype(F32)
+            into[pl.ds(off, step), :] = total.astype(BF16)
+
+    def scatter_on(key, m, at):
+        for copy in to_core[key]:
+            copy.wait_recv()
+        for d in range(1, pairs):
+            q = pair_at(d)
+            held = piece(grad, m, 2 * q + core, at)
+            combine(m, held, 2 * q + core, [from_core.at[m, q, :, at]], at)
+            to_pair[key][d - 1].start()
+
+    def scatter_home(key, m, at):
+        for copy in to_pair[key]:
+            copy.wait_recv()
+        terms = [from_core.at[m, pair, :, at]]
+        terms += [from_pair.at[m, d, :, at] for d in range(pairs - 1)]
+
+        @pl.when(leads)
+        def _():
+            combine(m, last.at[m, :, at], 2 * pair + core, terms, at)
+
+        @pl.when(moves)
+        def _():
+            combine(m, piece(grad, m, 2 * pair + core, at), 2 * pair + core, terms, at)
+            to_home[key].start()
+
+    def moved_on(key, m, at):
+        @pl.when(moves)
+        def _():
+            scatter_on(key, m, at)
+
+    def led_on(key, m, at):
+        @pl.when(leads)
+        def _():
+            scatter_on(key, m, at)
+
+    energy = zero
+    for t in range(tiles):
+        gathered(parts[t])
+        energy = classify(t, energy)
+        if t + 2 < tiles:
+            spread_moved(parts[t + 2])
+        product(2, resid_t, dlog, cols(t))
+        scatter((2, t), 2, cols(t))
+        if t + 1 < tiles:
+            forward(parts[t + 1], 2, cols(t + 1))
+        if t > 0:
+            moved_on((2, t - 1), 2, cols(t - 1))
+    moved_on((2, tiles - 1), 2, cols(tiles - 1))
+
+    power[0] = energy * (0.5 * norm)
+    power_swap = swap(power.at[0], power.at[1])
+    send(power_swap)
+
+    for t in range(tiles):
+        at = cols(t)
+        dres[:, at] = dot_nt(dlog[...], wide[2, at, :]).astype(BF16)
+        led_on((2, t), 2, at)
+        product(1, hid_t, dres, at)
+        scatter((1, t), 1, at)
+        if t > 0:
+            scatter_on((1, t - 1), 1, cols(t - 1))
 
     @pl.loop(0, tiles)
     def _(t):
         at = column(t)
         rows_t[at, :] = rows[:, at].T
 
-    gathered(0)
-
-    @pl.loop(0, tiles)
-    def _(t):
-        at = column(t)
-        pre = dot_nn(rows[...], wide[0, :, at])
-        sig = jax.nn.sigmoid(pre)
-        value = (pre * sig).astype(BF16)
-        hid[:, at] = value
-        hid_t[at, :] = value.T
-        slope[:, at] = sig * (1.0 + pre * (1.0 - sig))
-
-    spread(1, 1)
-    chunk(spread, 0)
-    forward(1, 1)
-    for t in range(1, tiles):
-        chunk(spread, t)
+    scatter_on((1, tiles - 1), 1, cols(tiles - 1))
+
+    for t in range(tiles):
+        at = cols(t)
+        dlog[:, at] = (dot_nt(dres[...], wide[1, at, :]) * slope[:, at]).astype(BF16)
+        product(0, rows_t, dlog, at)
+        scatter((0, t), 0, at)
+        if t > 0:
+            scatter_on((0, t - 1), 0, cols(t - 1))
+    scatter_on((0, tiles - 1), 0, cols(tiles - 1))
 
     for copy in sums_out:
         copy.wait_recv()
@@ -395,126 +560,6 @@
     spans_out = [
         begin(remote(spans.at[ci], spans.at[ci], (lax.rem(ci + d, c), me))) for d in range(1, c)
     ]
-
-    gathered(1)
-
-    @pl.loop(0, tiles)
-    def _(t):
-        at = column(t)
-        value = (rows[:, at].astype(F32) + dot_nn(hid[...], wide[1, :, at])).astype(BF16)
-        resid[:, at] = value
-        resid_t[at, :] = value.T
-
-    chunk(forward, 0)
-
-    def classify(t, energy):
-        at = column(t)
-        logits = dot_nn(resid[...], wide[2, :, at])
-        parts = []
-        for k in range(TILE // LANES):
-            target = (lab_t[...] == lane + (t * TILE + k * LANES)).astype(F32)
-            err = logits[:, k * LANES : (k + 1) * LANES] - target
-            energy = energy + fold(err * err)
-            parts.append((err * norm).astype(BF16))
-        dlog[:, at] = jnp.concatenate(parts, axis=1)
-        return energy
-
-    def products(m, left_t, right):
-        @pl.loop(0, depth // TILE)
-        def _(t):
-            at = column(t)
-            grad[m, at, :] = dot_nn(left_t[at, :], right[...]).astype(BF16)
-
-    to_core, to_pair, to_home = {}, {}, {}
-
-    def scatter(key, m, at=everything):
-        to_core[key] = [
-            begin(remote(piece(grad, m, 2 * q + 1 - core, at), from_core.at[m, q, :, at], twin))
-            for q in range(pairs)
-        ]
-
-    def combine(m, into, index, parts, cols=everything):
-        @pl.loop(0, block // step)
-        def _(r):
-            off = pl.multiple_of(r * step, step)
-            at = pl.ds(pl.multiple_of(index * block + off, step), step)
-            total = grad[m, at, cols].astype(F32)
-            for part in parts:
-                total = total + part[pl.ds(off, step), :].astype(F32)
-            into[pl.ds(off, step), :] = total.astype(BF16)
-
-    def scatter_on(key, m, at=everything):
-        for copy in to_core[key]:
-            copy.wait_recv()
-        to_pair.setdefault(m, [])
-        for d in range(1, pairs):
-            q = pair_at(d)
-            held = piece(grad, m, 2 * q + core, at)
-            combine(m, held, 2 * q + core, [from_core.at[m, q, :, at]], at)
-            to_pair[m].append(
-                begin(remote(held, from_pair.at[m, d - 1, :, at], (ci, 2 * q + side)))
-            )
-
-    def scatter_home(m):
-        for copy in to_pair[m]:
-            copy.wait_recv()
-        parts = [from_core.at[m, pair]] + [from_pair.at[m, d] for d in range(pairs - 1)]
-        held = piece(grad, m, 2 * pair + core)
-        combine(m, held, 2 * pair + core, parts)
-
-        @pl.when(leads)
-        def _():
-            @pl.loop(0, block // step)
-            def _(r):
-                off = pl.multiple_of(r * step, step)
-                at = pl.ds(pl.multiple_of(me * block + off, step), step)
-                last[m, pl.ds(off, step), :] = grad[m, at, :]
-
-        to_home[m] = swap(held, last.at[m])
-
-    energy = zero
-    for t in range(tiles):
-        if t + 1 < tiles:
-            chunk(forward, t + 1)
-        gathered((2, t))
-        energy = classify(t, energy)
-        at = pl.ds(t * TILE, TILE)
-
-        @pl.loop(0, depth // TILE)
-        def _(r):
-            of = column(r)
-            grad[2, of, at] = dot_nn(resid_t[of, :], dlog[:, at]).astype(BF16)
-
-        scatter((2, t), 2, at)
-        if t > 0:
-            chunk(scatter_on, t - 1)
-
-    @pl.loop(0, depth // TILE)
-    def _(t):
-        at = column(t)
-        dres[:, at] = dot_nt(dlog[...], wide[2, at, :]).astype(BF16)
-
-    chunk(scatter_on, tiles - 1)
-
-    products(1, hid_t, dres)
-    scatter(1, 1)
-
-    @pl.loop(0, depth // TILE)
-    def _(t):
-        at = column(t)
-        dlog[:, at] = (dot_nt(dres[...], wide[1, at, :]) * slope[:, at]).astype(BF16)
-
-    scatter_on(1, 1)
-    products(0, rows_t, dlog)
-    scatter(0, 0)
-    power[0] = energy * (0.5 * norm)
-    power_swap = swap(power.at[0], power.at[1])
-
-    scatter_on(0, 0)
-    scatter_home(2)
-
-    for copy in spans_out:
-        copy.wait_recv()
     by_ahead = 1.0 / (len_ahead * raw_len)
     by_behind = 1.0 / (len_behind * raw_len)
 
@@ -528,6 +573,8 @@
 
         lax.fori_loop(0, block // step, body, 0)
 
+    for copy in spans_out:
+        copy.wait_recv()
     arc = jnp.zeros((1, 1), F32)
     band = jnp.zeros((1, 1), F32)
     for k in range(c):
@@ -535,25 +582,29 @@
         arc = arc + jnp.where(k <= ci, length, 0.0)
         band = band + length
     band = band + spans[c - 1, 1, 0:1, 0:1]
-
-    for m in (1, 0):
-        scatter_home(m)
     arrive(power_swap)
 
-    def finish(m, carry):
-        arrive(to_home[m])
+    def finish(key, m, cs, carry):
+        arrive(to_home[key])
 
         def body(r, carry):
             at = pl.ds(pl.multiple_of(r * step, step), step)
-            total = last[m, at, :].astype(F32) * factor[m]
-            edge[m, at, :] = total
-            return carry[0] + fold(total * tau[m, at, :]), carry[1] + fold(total * total)
+            total = last[m, at, cs].astype(F32) * factor[m]
+            edge[m, at, cs] = total
+            return carry[0] + fold(total * tau[m, at, cs]), carry[1] + fold(total * total)
 
         return lax.fori_loop(0, block // step, body, carry)
 
     carry = (zero, zero)
-    for m in (2, 1, 0):
-        carry = finish(m, carry)
+    queue = [(m, t) for m in (2, 1, 0) for t in range(tiles)]
+    lag = 2
+    for i in range(len(queue) + lag):
+        if i < len(queue):
+            m, t = queue[i]
+            scatter_home((m, t), m, cols(t))
+        if i >= lag:
+            m, t = queue[i - lag]
+            carry = finish((m, t), m, cols(t), carry)
     late[me, 0] = carry[0]
     late[me, 1] = carry[1]
     late[me, 2] = jnp.where(leads, power[0], power[1])

time: 127 us -> 116 us (0.913); the launches traced: 125 us -> 116 us
  Pallas kernels: 114 us -> 105 us
    pallas_call x1, Pallas kernels: 114 us -> 105 us  [on_device(): pl.pallas_call(functools.partial(kernel, n, c, classes), out_shape=(jax.S...]
where the time goes in v1:
time: 116 us
  Pallas kernels  105 us (91%)
  between operations  6.5 us (6%)
  local copies, waits for them, and re-layouts  4.39 us (4%)
    pallas_call x1, Pallas kernels, on_device(): pl.pallas_call(functools.partial(kernel, n, c, classes), out_shape=(jax.S...  105 us
    unnamed x7, local copies, waits for them, and re-layouts  4.39 us

profile of v1, /device:TPU:0, one launch (start us, length us, event | category | flops | bytes accessed | tf_op | source)
XLA Modules:
  0.0 116.0 jit_solution(9543609914842129013)
XLA Ops:
  1.3 105.1 %shard_map.145 = (f32[1,256,1024]{2,1,0:T(8,128)}, f32[1,256,1024]{2,1,0:T(8,128)}, f32[1,1000,256]{2,1,0:T(8,128)}, f32[1]{0:T(128)}, f32[1]{0:T(128)}, /*index=5*/f32[1]{0:T(128)}) custom-call(f32[1,256,1024]{2,1,0:T(8,128)} %p_in.1, f32[1,256,1024]{2,1,0:T(8,128)} %p_mid.1, f32[1,1000,256]{2,1,0:T(8,128)} %bitcast.4, f32[2,256,1024]{2,1,0:T(8,128)} %e_in.1, ...), custom_call_target="tpu_custom_call" | custom-call | tf_op jit(solution)/shard_map/pallas_call | solution.py:696
  106.4 0.0 copy-start
  106.4 0.0 copy-start.1
  106.4 2.5 %copy.23 = f32[1,256,1024]{2,1,0:T(8,128)} copy(f32[1,256,1024]{2,1,0:T(8,128)} %get-tuple-element.24) | data formatting | bytes 2097152
  108.9 0.0 copy-done
  108.9 1.0 copy.24
  109.8 0.0 copy-done.1
  109.8 1.0 copy.25
Async XLA Ops:
  106.4 2.5 %copy-start = (f32[1,256,1024]{2,1,0:T(8,128)S(1)}, f32[1,256,1024]{2,1,0:T(8,128)}, u32[]{:S(2)}) copy-start(f32[1,256,1024]{2,1,0:T(8,128)} %get-tuple-element.25) | copy-start | bytes 3145732
  106.4 3.4 %copy-start.1 = (f32[1,1000,256]{2,1,0:T(8,128)S(1)}, f32[1,1000,256]{2,1,0:T(8,128)}, u32[]{:S(2)}) copy-start(f32[1,1000,256]{2,1,0:T(8,128)} %get-tuple-element.14) | copy-start | bytes 3072004

commit v2 on v1

--- a/solution.py
+++ b/solution.py
@@ -15,11 +15,11 @@
 BF16 = jnp.bfloat16
 
 
-def copies_of(count, chain, chunks):
+def copies_of(count, chain, chunks, rows):
     pairs = count // 2
-    gather = (2 + chunks) * (1 + (pairs - 1) + pairs)
+    gather = 3 * (1 + (pairs - 1) + pairs)
     scatter = 3 * chunks * (pairs + (pairs - 1) + 1)
-    return gather + scatter + 6 + 2 * (count - 1) + (chain - 1) + 2 + 2
+    return gather + scatter + 6 + 2 * (count - 1) + (chain - 1) + 2 + rows
 
 
 def dot_nn(left, right):
@@ -63,20 +63,17 @@
     o_in,
     o_mid,
     o_out,
-    o_energy,
-    o_arc,
-    o_bend,
+    o_small,
     own,
     edge,
     thin,
-    tau,
+    tau_out,
     wide,
     stage,
     near,
     before,
     after,
     pool_v,
-    hot,
     lab_t,
     lab_out,
     lab_in,
@@ -118,6 +115,7 @@
     factor = (depth**-0.5, width**-0.5, depth**-0.5)
     norm = 1.0 / (batch * n * classes)
     counter = [0]
+    tau = [o_in.at[0], o_mid.at[0], tau_out]
 
     def remote(src, dst, to):
         k = counter[0]
@@ -134,7 +132,6 @@
 
     def pair_at(d):
         return lax.rem(pair + d, pairs)
-
     barrier = pltpu.get_barrier_semaphore()
     for d in range(1, n):
         pl.semaphore_signal(
@@ -192,8 +189,8 @@
         return pl.ds(pl.multiple_of(t * TILE, TILE), TILE)
 
     everything = pl.ds(0, width)
-    tail = TILE if batch > TILE else 0
-    blocks = [pl.ds(0, batch - tail)] + ([pl.ds(batch - tail, tail)] if tail else [])
+    cuts = [0] + [at for at in (batch - 2 * TILE, batch - TILE) if at > 0] + [batch]
+    blocks = [pl.ds(low, high - low) for low, high in zip(cuts[:-1], cuts[1:])]
 
     def piece(ref, m, index, at=everything):
         return ref.at[m, pl.ds(pl.multiple_of(index * block, block), block), at]
@@ -264,12 +261,8 @@
     def cols(t):
         return pl.ds(t * TILE, TILE)
 
-    parts = [(2, t) for t in range(tiles)]
-    for m in range(2):
+    for m in range(3):
         prepare(m, m)
-    for key in parts:
-        prepare(key, 2, cols(key[1]))
-
     loads[0].wait()
     lowered(0)
     pl.semaphore_wait(barrier, n - 1 + c - 1 + 1)
@@ -284,7 +277,8 @@
     loads[2].wait()
     turned(own.at[2], 0)
     lowered(2)
-    spread_own(*parts)
+    send(hop[2])
+    spread_own(2)
 
     ups = [remote(near.at[m], before.at[m], (lax.rem(ci + 1, c), me)) for m in range(3)]
     downs = [remote(near.at[m], after.at[m], (lax.rem(ci + c - 1, c), me)) for m in range(3)]
@@ -299,7 +293,6 @@
     def _():
         for copy in downs:
             copy.start()
-
     lab_rows = jnp.broadcast_to(labs[...], (8, batch))
     lab_out[...] = lab_rows
 
@@ -311,8 +304,17 @@
     send(lab_swap)
     row_of = jnp.broadcast_to(picks[...], (LANES, batch)).T
     lane = lax.broadcasted_iota(jnp.int32, (batch, LANES), 1)
-    for k in range(pool_v.shape[0] // LANES):
-        hot[:, k * LANES : (k + 1) * LANES] = (row_of == lane + k * LANES).astype(F32).astype(BF16)
+    supply = pool_v.shape[0]
+    for k in range(supply // LANES):
+        m, at = k * LANES // width, k * LANES % width
+        grad[m, 0:batch, at : at + LANES] = (row_of == lane + k * LANES).astype(F32).astype(BF16)
+    reach = [(m, min(width, supply - m * width)) for m in range(-(-supply // width))]
+
+    def picked_of(rs, at):
+        return sum(
+            dot_nn(grad[m, rs, 0:size], pool_v[pl.ds(m * width, size), at]) for m, size in reach
+        )
+
     loads[3].wait()
     row_swap = []
     for b, rs in enumerate(blocks):
@@ -320,7 +322,7 @@
         @pl.loop(0, tiles)
         def _(t):
             at = column(t)
-            picked = dot_nn(hot[rs, :], pool_v[:, at]).astype(BF16)
+            picked = picked_of(rs, at).astype(BF16)
             rows_out[rs, at] = picked
 
             @pl.when(leads)
@@ -329,11 +331,7 @@
 
         row_swap.append(swap(rows_out.at[rs], rows.at[rs]))
         send(row_swap[b])
-        if b == 0:
-            send(hop[parts[0]])
-    send(*[hop[key] for key in parts[1:]])
-
-    spread_moved(0, 1)
+    spread_moved(0, 1, 2)
     forward(0, 0)
     for load in loads[4:]:
         load.wait()
@@ -355,7 +353,6 @@
         left = jnp.where(ci == 0, fixed, before[m, at, :].astype(F32))
         right = jnp.where(ci == c - 1, fixed, after[m, at, :].astype(F32))
         return right - mine, mine - left
-
     zero = jnp.zeros((8, LANES), F32)
 
     def span_sums(m, carry):
@@ -377,7 +374,6 @@
     sums_out = [
         begin(remote(sums.at[me], sums.at[me], (ci, lax.rem(me + d, n)))) for d in range(1, n)
     ]
-
     gathered(0)
     arrive(lab_swap)
     lab_t[...] = jnp.broadcast_to(lab_in[...][0:1, :], (LANES, batch)).T
@@ -402,17 +398,15 @@
             resid_t[at, rs] = value.T
 
     for b, rs in enumerate(blocks):
+        if b == len(blocks) - 1:
+            forward(2, 2)
         arrive(row_swap[b])
         activate(rs)
         if b == 0:
-            spread_moved(parts[0])
             forward(1, 1)
             gathered(1)
         residual(rs)
-
-    if tiles > 1:
-        spread_moved(parts[1])
-    forward(parts[0], 2, cols(0))
+    gathered(2)
 
     def classify(t, energy):
         at = column(t)
@@ -496,47 +490,15 @@
 
     energy = zero
     for t in range(tiles):
-        gathered(parts[t])
         energy = classify(t, energy)
-        if t + 2 < tiles:
-            spread_moved(parts[t + 2])
         product(2, resid_t, dlog, cols(t))
         scatter((2, t), 2, cols(t))
-        if t + 1 < tiles:
-            forward(parts[t + 1], 2, cols(t + 1))
         if t > 0:
             moved_on((2, t - 1), 2, cols(t - 1))
-    moved_on((2, tiles - 1), 2, cols(tiles - 1))
 
     power[0] = energy * (0.5 * norm)
     power_swap = swap(power.at[0], power.at[1])
     send(power_swap)
-
-    for t in range(tiles):
-        at = cols(t)
-        dres[:, at] = dot_nt(dlog[...], wide[2, at, :]).astype(BF16)
-        led_on((2, t), 2, at)
-        product(1, hid_t, dres, at)
-        scatter((1, t), 1, at)
-        if t > 0:
-            scatter_on((1, t - 1), 1, cols(t - 1))
-
-    @pl.loop(0, tiles)
-    def _(t):
-        at = column(t)
-        rows_t[at, :] = rows[:, at].T
-
-    scatter_on((1, tiles - 1), 1, cols(tiles - 1))
-
-    for t in range(tiles):
-        at = cols(t)
-        dlog[:, at] = (dot_nt(dres[...], wide[1, at, :]) * slope[:, at]).astype(BF16)
-        product(0, rows_t, dlog, at)
-        scatter((0, t), 0, at)
-        if t > 0:
-            scatter_on((0, t - 1), 0, cols(t - 1))
-    scatter_on((0, tiles - 1), 0, cols(tiles - 1))
-
     for copy in sums_out:
         copy.wait_recv()
 
@@ -563,16 +525,48 @@
     by_ahead = 1.0 / (len_ahead * raw_len)
     by_behind = 1.0 / (len_behind * raw_len)
 
+    for t in range(tiles):
+        at = cols(t)
+        dres[:, at] = dot_nt(dlog[...], wide[2, at, :]).astype(BF16)
+        if t == 0:
+            moved_on((2, tiles - 1), 2, cols(tiles - 1))
+        led_on((2, t), 2, at)
+        product(1, hid_t, dres, at)
+        scatter((1, t), 1, at)
+        if t > 0:
+            scatter_on((1, t - 1), 1, cols(t - 1))
+    @pl.loop(0, tiles)
+    def _(t):
+        at = column(t)
+        rows_t[at, :] = rows[:, at].T
+    scatter_on((1, tiles - 1), 1, cols(tiles - 1))
+
+    for t in range(tiles):
+        at = cols(t)
+        dlog[:, at] = (dot_nt(dres[...], wide[1, at, :]) * slope[:, at]).astype(BF16)
+        product(0, rows_t, dlog, at)
+        scatter((0, t), 0, at)
+        if t > 0:
+            scatter_on((0, t - 1), 0, cols(t - 1))
+
+        @pl.when(moves)
+        def _():
+            scatter_home((2, t), 2, at)
     for m in range(3):
 
         def body(r, _, m=m):
             at = pl.ds(pl.multiple_of(r * step, step), step)
             ahead, behind = differences(m, at)
-            tau[m, at, :] = ahead * by_ahead + behind * by_behind
+            tau[m][at, :] = ahead * by_ahead + behind * by_behind
             return 0
 
         lax.fori_loop(0, block // step, body, 0)
-
+    scatter_on((0, tiles - 1), 0, cols(tiles - 1))
+
+    @pl.when(leads)
+    def _():
+        for t in range(tiles):
+            scatter_home((2, t), 2, cols(t))
     for copy in spans_out:
         copy.wait_recv()
     arc = jnp.zeros((1, 1), F32)
@@ -591,19 +585,18 @@
             at = pl.ds(pl.multiple_of(r * step, step), step)
             total = last[m, at, cs].astype(F32) * factor[m]
             edge[m, at, cs] = total
-            return carry[0] + fold(total * tau[m, at, cs]), carry[1] + fold(total * total)
+            return carry[0] + fold(total * tau[m][at, cs]), carry[1] + fold(total * total)
 
         return lax.fori_loop(0, block // step, body, carry)
 
     carry = (zero, zero)
-    queue = [(m, t) for m in (2, 1, 0) for t in range(tiles)]
-    lag = 2
-    for i in range(len(queue) + lag):
-        if i < len(queue):
-            m, t = queue[i]
-            scatter_home((m, t), m, cols(t))
-        if i >= lag:
-            m, t = queue[i - lag]
+    for t in range(tiles):
+        scatter_home((1, t), 1, cols(t))
+    for i in range(tiles):
+        carry = finish((2, i), 2, cols(i), carry)
+        scatter_home((0, i), 0, cols(i))
+    for m in (1, 0):
+        for t in range(tiles):
             carry = finish((m, t), m, cols(t), carry)
     late[me, 0] = carry[0]
     late[me, 1] = carry[1]
@@ -621,33 +614,30 @@
     force_sq = g_g - 2.0 * coef * along + coef * coef * tau_sq
     scale = band / (c + 1) / jnp.sqrt(force_sq + EPS)
     push = scale * coef
-    o_energy[0] = energy_all[0, 0]
-    o_arc[0] = (arc / band)[0, 0]
-    o_bend[0] = (0.5 * raw_len)[0, 0]
-
-    stores = []
-    for m, out in ((2, o_out), (1, o_mid), (0, o_in)):
-        if m == 2:
-
-            @pl.loop(0, width // LANES)
-            def _(k):
-                at = pl.ds(pl.multiple_of(k * LANES, LANES), LANES)
-                new = own[2, :, at] + (push * tau[2, :, at] - scale * edge[2, :, at])
-                thin[0, at, :] = new.T
-
-            source = thin.at[0, pl.ds(0, classes)]
-        else:
-
-            @pl.loop(0, block // step)
-            def _(r):
-                at = pl.ds(pl.multiple_of(r * step, step), step)
-                tau[m, at, :] = own[m, at, :] + (push * tau[m, at, :] - scale * edge[m, at, :])
-
-            source = tau.at[m]
-        copy = pltpu.make_async_copy(source, out.at[0], load_sem.at[m])
-        copy.start()
-        stores.append(copy)
-
+    def small(value):
+        return jnp.broadcast_to(value, (1, LANES))
+
+    o_small[0:1, :] = small(energy_all)
+    o_small[1:2, :] = small(arc / band)
+    o_small[2:3, :] = small(0.5 * raw_len)
+    @pl.loop(0, classes // LANES)
+    def _(k):
+        at = pl.ds(pl.multiple_of(k * LANES, LANES), LANES)
+        new = own[2, :, at] + (push * tau_out[:, at] - scale * edge[2, :, at])
+        o_out[0, at, :] = new.T
+
+    rest = classes % LANES
+    if rest:
+        low = classes - rest
+        at = pl.ds(low, LANES)
+        new = own[2, :, at] + (push * tau_out[:, at] - scale * edge[2, :, at])
+        o_out[0, low:classes, :] = new.T[0:rest, :]
+    for m in range(2):
+
+        @pl.loop(0, block // step)
+        def _(r):
+            at = pl.ds(pl.multiple_of(r * step, step), step)
+            tau[m][at, :] = own[m, at, :] + (push * tau[m][at, :] - scale * edge[m, at, :])
     @pl.when(has_next)
     def _():
         for copy in ups:
@@ -665,8 +655,6 @@
 
     for copy in started:
         copy.wait_send()
-    for copy in stores:
-        copy.wait()
 
 
 def on_device(
@@ -688,35 +676,31 @@
     depth = n * block
     batch = batch_rows.shape[1]
     pairs = n // 2
-    copies = copies_of(n, c, width // TILE)
+    copies = copies_of(n, c, width // TILE, 3)
     vmem = pl.BlockSpec(memory_space=pltpu.VMEM)
     anywhere = pl.BlockSpec(memory_space=pl.ANY)
     scalar = pl.BlockSpec(memory_space=pltpu.SMEM)
-    small = jax.ShapeDtypeStruct((1,), F32)
     outs = pl.pallas_call(
         functools.partial(kernel, n, c, classes),
         out_shape=(
-            jax.ShapeDtypeStruct(images_in.shape, F32),
-            jax.ShapeDtypeStruct(images_mid.shape, F32),
-            jax.ShapeDtypeStruct((1, classes, block), F32),
-            small,
-            small,
-            small,
+            pltpu.VMEM(images_in.shape, F32),
+            pltpu.VMEM(images_mid.shape, F32),
+            pltpu.VMEM((1, classes, block), F32),
+            pltpu.VMEM((8, LANES), F32),
         ),
         in_specs=[anywhere] * 7 + [vmem] * 2 + [scalar],
-        out_specs=[anywhere] * 3 + [scalar] * 3,
+        out_specs=[vmem] * 4,
         scratch_shapes=[
             pltpu.VMEM((3, block, width), F32),
             pltpu.VMEM((3, block, width), F32),
             pltpu.VMEM((2, width, block), F32),
-            pltpu.VMEM((3, block, width), F32),
+            pltpu.VMEM((block, width), F32),
             pltpu.VMEM((3, depth, width), BF16),
             pltpu.VMEM((3, block, width), BF16),
             pltpu.VMEM((3, block, width), BF16),
             pltpu.VMEM((3, block, width), BF16),
             pltpu.VMEM((3, block, width), BF16),
             pltpu.VMEM(data_pool.shape, BF16),
-            pltpu.VMEM((batch, data_pool.shape[0]), BF16),
             pltpu.VMEM((batch, LANES), jnp.int32),
             pltpu.VMEM((8, batch), jnp.int32),
             pltpu.VMEM((8, batch), jnp.int32),
@@ -743,7 +727,7 @@
             pltpu.SemaphoreType.DMA((copies,)),
         ],
         compiler_params=pltpu.CompilerParams(
-            collective_id=0, has_side_effects=True, vmem_limit_bytes=63 * 1024 * 1024
+            collective_id=0, has_side_effects=True, vmem_limit_bytes=60 * 1024 * 1024
         ),
     )(
         images_in,
@@ -757,7 +741,7 @@
         labels,
         climbing,
     )
-    return (outs[0], outs[1], jnp.swapaxes(outs[2], 1, 2), *outs[3:])
+    return (outs[0], outs[1], jnp.swapaxes(outs[2], 1, 2), *(outs[3][k, 0:1] for k in range(3)))
 
 
 def solution(mesh):

time: 116 us -> 102 us (0.88)
  Pallas kernels: 105 us -> 96.7 us
  between operations: 6.5 us -> 1.29 us
    pallas_call x1, Pallas kernels: 105 us -> 96.7 us  [on_device(): pl.pallas_call(functools.partial(kernel, n, c, classes), out_shape=(pltpu...]
    unnamed x7 -> x3, local copies, waits for them, and re-layouts: 4.39 us -> 2.9 us
where the time goes in v2:
time: 102 us; the launch traced here: 101 us
  Pallas kernels  96.7 us (95%)
  local copies, waits for them, and re-layouts  3.42 us (3%)
  between operations  1.29 us (1%)
    pallas_call x1, Pallas kernels, on_device(): pl.pallas_call(functools.partial(kernel, n, c, classes), out_shape=(pltpu...  96.7 us
    unnamed x3, local copies, waits for them, and re-layouts  2.9 us

profile of v2, /device:TPU:0, one launch (start us, length us, event | category | flops | bytes accessed | tf_op | source)
XLA Modules:
  0.0 101.4 jit_solution(7599435660540395912)
XLA Ops:
  1.3 96.7 %shard_map.145 = (f32[1,256,1024]{2,1,0:T(8,128)S(1)}, f32[1,256,1024]{2,1,0:T(8,128)S(1)}, f32[1,1000,256]{2,1,0:T(8,128)S(1)}, f32[8,128]{1,0:T(8,128)S(1)}) custom-call(f32[1,256,1024]{2,1,0:T(8,128)} %p_in.1, f32[1,256,1024]{2,1,0:T(8,128)} %p_mid.1, f32[1,1000,256]{2,1,0:T(8,128)} %bitcast.8, f32[2,256,1024]{2,1,0:T(8,128)} %e_in.1, ...), custom_call_target="tpu_custom_call" | custom-call | tf_op jit(solution)/shard_map/pallas_call | solution.py:683
  98.0 0.5 fusion
  98.5 1.0 copy.19
  99.5 1.0 copy.20
  100.5 1.0 copy.21

commit v3 on v2

--- a/solution.py
+++ b/solution.py
@@ -19,7 +19,7 @@
     pairs = count // 2
     gather = 3 * (1 + (pairs - 1) + pairs)
     scatter = 3 * chunks * (pairs + (pairs - 1) + 1)
-    return gather + scatter + 6 + 2 * (count - 1) + (chain - 1) + 2 + rows
+    return gather + scatter + 6 + 2 * (count - 1) + (chain - 1) + 2 + rows + chain // 2
 
 
 def dot_nn(left, right):
@@ -74,6 +74,7 @@
     before,
     after,
     pool_v,
+    pool_x,
     lab_t,
     lab_out,
     lab_in,
@@ -154,8 +155,8 @@
         pltpu.make_async_copy(e_mid.at[end], edge.at[1], load_sem.at[5]),
         pltpu.make_async_copy(e_out.at[end], thin.at[1, pl.ds(0, classes)], load_sem.at[6]),
     ]
-    for load in loads:
-        load.start()
+    for k in (0, 3, 1, 2, 4, 5, 6):
+        loads[k].start()
 
     def turned(into, thin_at):
         @pl.loop(0, width // LANES)
@@ -188,7 +189,7 @@
     def column(t):
         return pl.ds(pl.multiple_of(t * TILE, TILE), TILE)
 
-    everything = pl.ds(0, width)
+    everything, everyone = pl.ds(0, width), pl.ds(0, batch)
     cuts = [0] + [at for at in (batch - 2 * TILE, batch - TILE) if at > 0] + [batch]
     blocks = [pl.ds(low, high - low) for low, high in zip(cuts[:-1], cuts[1:])]
 
@@ -266,7 +267,17 @@
     loads[0].wait()
     lowered(0)
     pl.semaphore_wait(barrier, n - 1 + c - 1 + 1)
-    send(hop[0])
+    planes, plane = c // 2, ci // 2
+    share = pool_v.shape[0] // planes
+    mine = pl.ds(pl.multiple_of(plane * share, share), share)
+    beyond = pl.ds(width - pool_x.shape[1], pool_x.shape[1])
+    pool_swap = swap(pool_v.at[mine, beyond], pool_x.at[mine])
+    pool_out = [
+        remote(pool_x.at[mine], pool_x.at[mine], (lax.rem(ci + 2 * d, c), me))
+        for d in range(1, planes)
+    ]
+    loads[3].wait()
+    send(pool_swap, hop[0])
     spread_own(0)
     loads[1].wait()
     lowered(1)
@@ -279,73 +290,68 @@
     lowered(2)
     send(hop[2])
     spread_own(2)
-
-    ups = [remote(near.at[m], before.at[m], (lax.rem(ci + 1, c), me)) for m in range(3)]
-    downs = [remote(near.at[m], after.at[m], (lax.rem(ci + c - 1, c), me)) for m in range(3)]
-    has_next, has_prev = ci < c - 1, ci > 0
-
-    @pl.when(has_next)
-    def _():
-        for copy in ups:
-            copy.start()
-
-    @pl.when(has_prev)
-    def _():
-        for copy in downs:
-            copy.start()
-    lab_rows = jnp.broadcast_to(labs[...], (8, batch))
-    lab_out[...] = lab_rows
+    lab_out[0] = jnp.broadcast_to(labs[...], (8, batch))
+    lab_out[1] = jnp.broadcast_to(picks[...], (8, batch))
 
     @pl.when(leads)
     def _():
-        lab_in[...] = lab_rows
+        lab_in[0] = lab_out[0]
 
     lab_swap = swap(lab_out, lab_in)
     send(lab_swap)
-    row_of = jnp.broadcast_to(picks[...], (LANES, batch)).T
     lane = lax.broadcasted_iota(jnp.int32, (batch, LANES), 1)
     supply = pool_v.shape[0]
-    for k in range(supply // LANES):
-        m, at = k * LANES // width, k * LANES % width
-        grad[m, 0:batch, at : at + LANES] = (row_of == lane + k * LANES).astype(F32).astype(BF16)
     reach = [(m, min(width, supply - m * width)) for m in range(-(-supply // width))]
 
-    def picked_of(rs, at):
+    def choose(row_of):
+        for k in range(supply // LANES):
+            m, at = k * LANES // width, k * LANES % width
+            grad[m, 0:batch, at : at + LANES] = (
+                (row_of == lane + k * LANES).astype(F32).astype(BF16)
+            )
+
+    def picked_of(rs, source, at):
         return sum(
-            dot_nn(grad[m, rs, 0:size], pool_v[pl.ds(m * width, size), at]) for m, size in reach
-        )
-
-    loads[3].wait()
+            dot_nn(grad[m, rs, 0:size], source[pl.ds(m * width, size), at]) for m, size in reach
+        ).astype(BF16)
+
+    choose(jnp.broadcast_to(picks[...], (LANES, batch)).T)
+    direct = width - pool_x.shape[1]
     row_swap = []
-    for b, rs in enumerate(blocks):
-
-        @pl.loop(0, tiles)
-        def _(t):
-            at = column(t)
-            picked = picked_of(rs, at).astype(BF16)
-            rows_out[rs, at] = picked
+    for rs in blocks:
+        for k in range(direct // TILE):
+            picked = picked_of(rs, pool_v, cols(k))
+            rows_out[rs, cols(k)] = picked
 
             @pl.when(leads)
             def _():
-                rows[rs, at] = picked
-
-        row_swap.append(swap(rows_out.at[rs], rows.at[rs]))
-        send(row_swap[b])
+                rows[rs, cols(k)] = picked
+
+        row_swap.append(swap(rows_out.at[rs, 0:direct], rows.at[rs, 0:direct]))
+        send(row_swap[-1])
+    @pl.when(leads)
+    def _():
+        for k in range(direct // TILE, tiles):
+            rows[:, cols(k)] = picked_of(everyone, pool_v, cols(k))
+
+    @pl.when(moves)
+    def _():
+        pool_swap.wait_recv()
+
+        @pl.when(plane < planes // 2)
+        def _():
+            for copy in pool_out[::-1]:
+                copy.start()
+
+        @pl.when(plane >= planes // 2)
+        def _():
+            for copy in pool_out:
+                copy.start()
     spread_moved(0, 1, 2)
     forward(0, 0)
     for load in loads[4:]:
         load.wait()
     turned(edge.at[2], 1)
-
-    @pl.when(has_prev)
-    def _():
-        for copy in ups:
-            copy.wait_recv()
-
-    @pl.when(has_next)
-    def _():
-        for copy in downs:
-            copy.wait_recv()
 
     def differences(m, at):
         mine = own[m, at, :]
@@ -353,35 +359,24 @@
         left = jnp.where(ci == 0, fixed, before[m, at, :].astype(F32))
         right = jnp.where(ci == c - 1, fixed, after[m, at, :].astype(F32))
         return right - mine, mine - left
+
     zero = jnp.zeros((8, LANES), F32)
-
-    def span_sums(m, carry):
-        def body(r, carry):
-            ahead, behind = differences(m, pl.ds(pl.multiple_of(r * step, step), step))
-            return (
-                carry[0] + fold(ahead * ahead),
-                carry[1] + fold(behind * behind),
-                carry[2] + fold(ahead * behind),
-            )
-
-        return lax.fori_loop(0, block // step, body, carry)
-
-    carry = (zero, zero, zero)
-    for m in range(3):
-        carry = span_sums(m, carry)
-    for k in range(3):
-        sums[me, k] = carry[k]
-    sums_out = [
-        begin(remote(sums.at[me], sums.at[me], (ci, lax.rem(me + d, n)))) for d in range(1, n)
-    ]
+    arrive(lab_swap)
+    lab_t[...] = jnp.broadcast_to(lab_in[0][0:1, :], (LANES, batch)).T
+    @pl.when(moves)
+    def _():
+        choose(jnp.broadcast_to(lab_in[1][0:1, :], (LANES, batch)).T)
+        for copy in pool_out:
+            copy.wait_recv()
+    @pl.when(moves)
+    def _():
+        for k in range(direct // TILE, tiles):
+            rows[:, cols(k)] = picked_of(everyone, pool_x, cols(k - direct // TILE))
     gathered(0)
-    arrive(lab_swap)
-    lab_t[...] = jnp.broadcast_to(lab_in[...][0:1, :], (LANES, batch)).T
 
     def activate(rs):
-        @pl.loop(0, tiles)
-        def _(t):
-            at = column(t)
+        for t in range(tiles):
+            at = cols(t)
             pre = dot_nn(rows[rs, :], wide[0, :, at])
             sig = jax.nn.sigmoid(pre)
             value = (pre * sig).astype(BF16)
@@ -390,21 +385,34 @@
             slope[rs, at] = sig * (1.0 + pre * (1.0 - sig))
 
     def residual(rs):
-        @pl.loop(0, tiles)
-        def _(t):
-            at = column(t)
+        for t in range(tiles):
+            at = cols(t)
             value = (rows[rs, at].astype(F32) + dot_nn(hid[rs, :], wide[1, :, at])).astype(BF16)
             resid[rs, at] = value
             resid_t[at, rs] = value.T
 
+    ups = [remote(near.at[m], before.at[m], (lax.rem(ci + 1, c), me)) for m in range(3)]
+    downs = [remote(near.at[m], after.at[m], (lax.rem(ci + c - 1, c), me)) for m in range(3)]
+    has_next, has_prev = ci < c - 1, ci > 0
+
     for b, rs in enumerate(blocks):
-        if b == len(blocks) - 1:
-            forward(2, 2)
         arrive(row_swap[b])
         activate(rs)
         if b == 0:
             forward(1, 1)
             gathered(1)
+            @pl.when(has_next)
+            def _():
+                for copy in ups:
+                    copy.start()
+
+            @pl.when(has_prev)
+            def _():
+                for copy in downs:
+                    copy.start()
+
+        if b == len(blocks) - 1:
+            forward(2, 2)
         residual(rs)
     gathered(2)
 
@@ -499,6 +507,84 @@
     power[0] = energy * (0.5 * norm)
     power_swap = swap(power.at[0], power.at[1])
     send(power_swap)
+
+    for t in range(tiles):
+        at = cols(t)
+        dres[:, at] = dot_nt(dlog[...], wide[2, at, :]).astype(BF16)
+        if t == 0:
+            moved_on((2, tiles - 1), 2, cols(tiles - 1))
+        led_on((2, t), 2, at)
+        product(1, hid_t, dres, at)
+        scatter((1, t), 1, at)
+        if t > 0:
+            scatter_on((1, t - 1), 1, cols(t - 1))
+    @pl.when(has_prev)
+    def _():
+        for copy in ups:
+            copy.wait_recv()
+
+    @pl.when(has_next)
+    def _():
+        for copy in downs:
+            copy.wait_recv()
+
+    def span_sums(m, carry):
+        def body(r, carry):
+            ahead, behind = differences(m, pl.ds(pl.multiple_of(r * step, step), step))
+            return (
+                carry[0] + fold(ahead * ahead),
+                carry[1] + fold(behind * behind),
+                carry[2] + fold(ahead * behind),
+            )
+
+        return lax.fori_loop(0, block // step, body, carry)
+
+    carry = (zero, zero, zero)
+    for m in range(3):
+        carry = span_sums(m, carry)
+    for k in range(3):
+        sums[me, k] = carry[k]
+    sums_out = [
+        begin(remote(sums.at[me], sums.at[me], (ci, lax.rem(me + d, n)))) for d in range(1, n)
+    ]
+    @pl.loop(0, tiles)
+    def _(t):
+        at = column(t)
+        rows_t[at, :] = rows[:, at].T
+    scatter_on((1, tiles - 1), 1, cols(tiles - 1))
+
+    for t in range(tiles):
+        at = cols(t)
+        dlog[:, at] = (dot_nt(dres[...], wide[1, at, :]) * slope[:, at]).astype(BF16)
+        product(0, rows_t, dlog, at)
+        scatter((0, t), 0, at)
+        if t > 0:
+            scatter_on((0, t - 1), 0, cols(t - 1))
+
+        @pl.when(moves)
+        def _():
+            scatter_home((2, t), 2, at)
+    scatter_on((0, tiles - 1), 0, cols(tiles - 1))
+
+    @pl.when(leads)
+    def _():
+        for t in range(tiles):
+            scatter_home((2, t), 2, cols(t))
+
+    def finish(key, m, cs, carry):
+        arrive(to_home[key])
+
+        def body(r, carry):
+            at = pl.ds(pl.multiple_of(r * step, step), step)
+            total = last[m, at, cs].astype(F32) * factor[m]
+            edge[m, at, cs] = total
+            return carry[0] + fold(total * tau[m][at, cs]), carry[1] + fold(total * total)
+
+        return lax.fori_loop(0, block // step, body, carry)
+
+    carry = (zero, zero)
+    for t in range(tiles):
+        scatter_home((1, t), 1, cols(t))
     for copy in sums_out:
         copy.wait_recv()
 
@@ -524,34 +610,6 @@
     ]
     by_ahead = 1.0 / (len_ahead * raw_len)
     by_behind = 1.0 / (len_behind * raw_len)
-
-    for t in range(tiles):
-        at = cols(t)
-        dres[:, at] = dot_nt(dlog[...], wide[2, at, :]).astype(BF16)
-        if t == 0:
-            moved_on((2, tiles - 1), 2, cols(tiles - 1))
-        led_on((2, t), 2, at)
-        product(1, hid_t, dres, at)
-        scatter((1, t), 1, at)
-        if t > 0:
-            scatter_on((1, t - 1), 1, cols(t - 1))
-    @pl.loop(0, tiles)
-    def _(t):
-        at = column(t)
-        rows_t[at, :] = rows[:, at].T
-    scatter_on((1, tiles - 1), 1, cols(tiles - 1))
-
-    for t in range(tiles):
-        at = cols(t)
-        dlog[:, at] = (dot_nt(dres[...], wide[1, at, :]) * slope[:, at]).astype(BF16)
-        product(0, rows_t, dlog, at)
-        scatter((0, t), 0, at)
-        if t > 0:
-            scatter_on((0, t - 1), 0, cols(t - 1))
-
-        @pl.when(moves)
-        def _():
-            scatter_home((2, t), 2, at)
     for m in range(3):
 
         def body(r, _, m=m):
@@ -561,12 +619,20 @@
             return 0
 
         lax.fori_loop(0, block // step, body, 0)
-    scatter_on((0, tiles - 1), 0, cols(tiles - 1))
-
-    @pl.when(leads)
-    def _():
+
+    for i in range(tiles):
+        carry = finish((2, i), 2, cols(i), carry)
+        scatter_home((0, i), 0, cols(i))
+    for m in (1, 0):
         for t in range(tiles):
-            scatter_home((2, t), 2, cols(t))
+            carry = finish((m, t), m, cols(t), carry)
+    arrive(power_swap)
+    late[me, 0] = carry[0]
+    late[me, 1] = carry[1]
+    late[me, 2] = jnp.where(leads, power[0], power[1])
+    late_out = [
+        begin(remote(late.at[me], late.at[me], (ci, lax.rem(me + d, n)))) for d in range(1, n)
+    ]
     for copy in spans_out:
         copy.wait_recv()
     arc = jnp.zeros((1, 1), F32)
@@ -576,34 +642,6 @@
         arc = arc + jnp.where(k <= ci, length, 0.0)
         band = band + length
     band = band + spans[c - 1, 1, 0:1, 0:1]
-    arrive(power_swap)
-
-    def finish(key, m, cs, carry):
-        arrive(to_home[key])
-
-        def body(r, carry):
-            at = pl.ds(pl.multiple_of(r * step, step), step)
-            total = last[m, at, cs].astype(F32) * factor[m]
-            edge[m, at, cs] = total
-            return carry[0] + fold(total * tau[m][at, cs]), carry[1] + fold(total * total)
-
-        return lax.fori_loop(0, block // step, body, carry)
-
-    carry = (zero, zero)
-    for t in range(tiles):
-        scatter_home((1, t), 1, cols(t))
-    for i in range(tiles):
-        carry = finish((2, i), 2, cols(i), carry)
-        scatter_home((0, i), 0, cols(i))
-    for m in (1, 0):
-        for t in range(tiles):
-            carry = finish((m, t), m, cols(t), carry)
-    late[me, 0] = carry[0]
-    late[me, 1] = carry[1]
-    late[me, 2] = jnp.where(leads, power[0], power[1])
-    late_out = [
-        begin(remote(late.at[me], late.at[me], (ci, lax.rem(me + d, n)))) for d in range(1, n)
-    ]
     for copy in late_out:
         copy.wait_recv()
     along, g_g, energy_all = (over_dp(late, k) for k in range(3))
@@ -650,7 +688,7 @@
 
     @pl.when(moves)
     def _():
-        for copy in swapped:
+        for copy in swapped + pool_out:
             copy.wait_send()
 
     for copy in started:
@@ -701,9 +739,10 @@
             pltpu.VMEM((3, block, width), BF16),
             pltpu.VMEM((3, block, width), BF16),
             pltpu.VMEM(data_pool.shape, BF16),
+            pltpu.VMEM((data_pool.shape[0], width // 2), BF16),
             pltpu.VMEM((batch, LANES), jnp.int32),
-            pltpu.VMEM((8, batch), jnp.int32),
-            pltpu.VMEM((8, batch), jnp.int32),
+            pltpu.VMEM((2, 8, batch), jnp.int32),
+            pltpu.VMEM((2, 8, batch), jnp.int32),
             pltpu.VMEM((batch, depth), BF16),
             pltpu.VMEM((batch, depth), BF16),
             pltpu.VMEM((batch, width), F32),

time: 102 us -> 95.7 us (0.938)
  Pallas kernels: 96.7 us -> 90.8 us
    pallas_call x1, Pallas kernels: 96.7 us -> 90.8 us  [on_device(): pl.pallas_call(functools.partial(kernel, n, c, classes), out_shape=(pltpu...]
where the time goes in v3:
time: 95.7 us; the launch traced here: 95.5 us
  Pallas kernels  90.8 us (95%)
  local copies, waits for them, and re-layouts  3.42 us (4%)
  between operations  1.29 us (1%)
    pallas_call x1, Pallas kernels, on_device(): pl.pallas_call(functools.partial(kernel, n, c, classes), out_shape=(pltpu...  90.8 us
    unnamed x3, local copies, waits for them, and re-layouts  2.9 us

profile of v3, /device:TPU:0, one launch (start us, length us, event | category | flops | bytes accessed | tf_op | source)
XLA Modules:
  0.0 95.5 jit_solution(4799215432222888513)
XLA Ops:
  1.3 90.8 %shard_map.145 = (f32[1,256,1024]{2,1,0:T(8,128)S(1)}, f32[1,256,1024]{2,1,0:T(8,128)S(1)}, f32[1,1000,256]{2,1,0:T(8,128)S(1)}, f32[8,128]{1,0:T(8,128)S(1)}) custom-call(f32[1,256,1024]{2,1,0:T(8,128)} %p_in.1, f32[1,256,1024]{2,1,0:T(8,128)} %p_mid.1, f32[1,1000,256]{2,1,0:T(8,128)} %bitcast.8, f32[2,256,1024]{2,1,0:T(8,128)} %e_in.1, ...), custom_call_target="tpu_custom_call" | custom-call | tf_op jit(solution)/shard_map/pallas_call | solution.py:721
  92.1 0.5 fusion
  92.6 1.0 %copy.19 = f32[1,256,1024]{2,1,0:T(8,128)} copy(f32[1,256,1024]{2,1,0:T(8,128)S(1)} %get-tuple-element.17) | data formatting | bytes 2097152
  93.6 1.0 %copy.20 = f32[1,256,1024]{2,1,0:T(8,128)} copy(f32[1,256,1024]{2,1,0:T(8,128)S(1)} %get-tuple-element.18) | data formatting | bytes 2097152
  94.5 1.0 %copy.21 = f32[1,256,1000]{1,2,0:T(8,128)} copy(f32[1,256,1000]{1,2,0:T(8,128)S(1)} %bitcast.6) | data formatting | bytes 2048000

commit v4 on v3

--- a/solution.py
+++ b/solution.py
@@ -15,11 +15,11 @@
 BF16 = jnp.bfloat16
 
 
-def copies_of(count, chain, chunks, rows):
+def semaphores(count, chunks, rows):
     pairs = count // 2
-    gather = 3 * (1 + (pairs - 1) + pairs)
-    scatter = 3 * chunks * (pairs + (pairs - 1) + 1)
-    return gather + scatter + 6 + 2 * (count - 1) + (chain - 1) + 2 + rows + chain // 2
+    sends = 1 + (pairs - 1) + pairs + 2 + 5 + 3 + 1 + (pairs - 1) + 1 + 1
+    receives = (2 + chunks) * ((pairs - 1) + pairs) + 3 + 2 + 4 + rows + 3 + 9 * chunks + 3 + 1
+    return sends, receives
 
 
 def dot_nn(left, right):
@@ -115,21 +115,28 @@
     tiles = width // TILE
     factor = (depth**-0.5, width**-0.5, depth**-0.5)
     norm = 1.0 / (batch * n * classes)
-    counter = [0]
+    counts = [0, 0]
     tau = [o_in.at[0], o_mid.at[0], tau_out]
 
-    def remote(src, dst, to):
-        k = counter[0]
-        counter[0] += 1
-        copy = pltpu.make_async_remote_copy(
+    def ticket(kind):
+        counts[kind] += 1
+        return counts[kind] - 1
+
+    def remote(src, dst, to, out=None, into=None):
+        return pltpu.make_async_remote_copy(
             src_ref=src,
             dst_ref=dst,
-            send_sem=send_sem.at[k],
-            recv_sem=recv_sem.at[k],
+            send_sem=send_sem.at[ticket(0) if out is None else out],
+            recv_sem=recv_sem.at[ticket(1) if into is None else into],
             device_id=to,
             device_id_type=pl.DeviceIdType.MESH,
         )
-        return copy
+
+    def sent(ref, out):
+        remote(ref, ref, twin, out, 0).wait_send()
+
+    def landed(ref, into):
+        remote(ref, ref, twin, 0, into).wait_recv()
 
     def pair_at(d):
         return lax.rem(pair + d, pairs)
@@ -146,17 +153,31 @@
     pl.semaphore_signal(barrier, inc=1, device_id=cross, device_id_type=pl.DeviceIdType.MESH)
 
     end = jnp.where(ci == 0, 0, 1)
+    planes, plane = c // 2, ci // 2
+    share = pool_v.shape[0] // planes
+    mine = pl.ds(pl.multiple_of(plane * share, share), share)
+
+    def load(k, src, dst):
+        return pltpu.make_async_copy(src, dst, load_sem.at[k])
+
+    def pool_rows(d):
+        return pl.ds(pl.multiple_of(lax.rem(plane + d, planes) * share, share), share)
+
     loads = [
-        pltpu.make_async_copy(p_in.at[0], own.at[0], load_sem.at[0]),
-        pltpu.make_async_copy(p_mid.at[0], own.at[1], load_sem.at[1]),
-        pltpu.make_async_copy(p_out.at[0], thin.at[0, pl.ds(0, classes)], load_sem.at[2]),
-        pltpu.make_async_copy(pool, pool_v, load_sem.at[3]),
-        pltpu.make_async_copy(e_in.at[end], edge.at[0], load_sem.at[4]),
-        pltpu.make_async_copy(e_mid.at[end], edge.at[1], load_sem.at[5]),
-        pltpu.make_async_copy(e_out.at[end], thin.at[1, pl.ds(0, classes)], load_sem.at[6]),
+        load(0, p_in.at[0], own.at[0]),
+        load(1, p_mid.at[0], own.at[1]),
+        load(2, p_out.at[0], thin.at[0, pl.ds(0, classes)]),
+        load(3, e_in.at[end], edge.at[0]),
+        load(4, e_mid.at[end], edge.at[1]),
+        load(5, e_out.at[end], thin.at[1, pl.ds(0, classes)]),
     ]
-    for k in (0, 3, 1, 2, 4, 5, 6):
-        loads[k].start()
+    pool_loads = [
+        load(6 + d, pool.at[pool_rows(d)], pool_v.at[pool_rows(d)]) for d in range(planes)
+    ]
+    for copy in (
+        [pool_loads[0], loads[0]] + loads[1:3] + pool_loads[1:] + loads[3:6]
+    ):
+        copy.start()
 
     def turned(into, thin_at):
         @pl.loop(0, width // LANES)
@@ -190,26 +211,15 @@
         return pl.ds(pl.multiple_of(t * TILE, TILE), TILE)
 
     everything, everyone = pl.ds(0, width), pl.ds(0, batch)
-    cuts = [0] + [at for at in (batch - 2 * TILE, batch - TILE) if at > 0] + [batch]
+    cuts = [0] + [at for at in (batch - 4 * LANES, batch - LANES) if at > 0] + [batch]
     blocks = [pl.ds(low, high - low) for low, high in zip(cuts[:-1], cuts[1:])]
 
     def piece(ref, m, index, at=everything):
         return ref.at[m, pl.ds(pl.multiple_of(index * block, block), block), at]
 
-    started = []
-
-    def begin(copy):
-        copy.start()
-        started.append(copy)
-        return copy
-
     hop, across, over = {}, {}, {}
-    swapped = []
-
-    def swap(src, dst):
-        copy = remote(src, dst, cross)
-        swapped.append(copy)
-        return copy
+    def swap(src, dst, out=None):
+        return remote(src, dst, cross, out)
 
     def send(*copies):
         @pl.when(moves)
@@ -223,14 +233,35 @@
             for copy in copies:
                 copy.wait_recv()
 
-    def prepare(key, m, at=everything):
-        hop[key] = swap(stage.at[m, :, at], piece(wide, m, me, at))
-        held = piece(wide, m, 2 * pair + core, at)
-        across[key] = [
-            remote(held, held, (ci, 2 * pair_at(d) + side)) for d in range(1, pairs)
+    hop_out = ticket(0)
+    across_out = [ticket(0) for _ in range(1, pairs)]
+    over_out = [ticket(0) for _ in range(pairs)]
+
+    def prepare(m):
+        hop[m] = swap(stage.at[m], piece(wide, m, me), hop_out)
+        held = piece(wide, m, 2 * pair + core)
+        across[m] = [
+            remote(held, held, (ci, 2 * pair_at(d) + side), across_out[d - 1])
+            for d in range(1, pairs)
         ]
-        over[key] = [remote(held, held, twin)]
-        started.extend(across[key] + over[key])
+        over[m] = [remote(held, held, twin, over_out[0])]
+        for d in range(1, pairs):
+            held = piece(wide, m, 2 * pair_at(pairs - d) + core)
+            over[m].append(remote(held, held, twin, over_out[d]))
+
+    parts = [(2, t) for t in range(tiles)]
+
+    def prepare_part(t):
+        at = cols(t)
+        held = piece(wide, 2, 2 * pair + core, at)
+        across[2, t] = [
+            remote(held, held, (ci, 2 * pair_at(d) + side), across_out[d - 1])
+            for d in range(1, pairs)
+        ]
+        over[2, t] = [remote(held, held, twin, over_out[0])]
+        for d in range(1, pairs):
+            held = piece(wide, 2, 2 * pair_at(pairs - d) + core, at)
+            over[2, t].append(remote(held, held, twin, over_out[d]))
 
     def spread(key):
         for copy in across[key] + over[key][:1]:
@@ -247,13 +278,13 @@
         def _():
             for key in keys:
                 hop[key].wait_recv()
-                spread(key)
-
-    def forward(key, m, at=everything):
+                for part in parts if key == 2 else [key]:
+                    spread(part)
+
+    def forward(key):
         for d in range(1, pairs):
             across[key][d - 1].wait_recv()
-            held = piece(wide, m, 2 * pair_at(pairs - d) + core, at)
-            over[key].append(begin(remote(held, held, twin)))
+            over[key][d].start()
 
     def gathered(key):
         for copy in over[key]:
@@ -262,21 +293,25 @@
     def cols(t):
         return pl.ds(t * TILE, TILE)
 
-    for m in range(3):
-        prepare(m, m)
+    for m in range(2):
+        prepare(m)
+    hop[2] = swap(stage.at[2], piece(wide, 2, me), hop_out)
+    for t in range(tiles):
+        prepare_part(t)
     loads[0].wait()
     lowered(0)
     pl.semaphore_wait(barrier, n - 1 + c - 1 + 1)
-    planes, plane = c // 2, ci // 2
-    share = pool_v.shape[0] // planes
-    mine = pl.ds(pl.multiple_of(plane * share, share), share)
     beyond = pl.ds(width - pool_x.shape[1], pool_x.shape[1])
     pool_swap = swap(pool_v.at[mine, beyond], pool_x.at[mine])
+    pool_sent, pool_landed = ticket(0), ticket(1)
     pool_out = [
-        remote(pool_x.at[mine], pool_x.at[mine], (lax.rem(ci + 2 * d, c), me))
+        remote(
+            pool_x.at[mine], pool_x.at[mine], (lax.rem(ci + 2 * d, c), me), pool_sent, pool_landed
+        )
         for d in range(1, planes)
     ]
-    loads[3].wait()
+    others = pool_x.at[pl.ds(0, (planes - 1) * share)]
+    pool_loads[0].wait()
     send(pool_swap, hop[0])
     spread_own(0)
     loads[1].wait()
@@ -289,7 +324,7 @@
     turned(own.at[2], 0)
     lowered(2)
     send(hop[2])
-    spread_own(2)
+    spread_own(*parts)
     lab_out[0] = jnp.broadcast_to(labs[...], (8, batch))
     lab_out[1] = jnp.broadcast_to(picks[...], (8, batch))
 
@@ -316,8 +351,10 @@
         ).astype(BF16)
 
     choose(jnp.broadcast_to(picks[...], (LANES, batch)).T)
+    for copy in pool_loads[1:]:
+        copy.wait()
     direct = width - pool_x.shape[1]
-    row_swap = []
+    row_swap, row_sent = [], ticket(0)
     for rs in blocks:
         for k in range(direct // TILE):
             picked = picked_of(rs, pool_v, cols(k))
@@ -327,7 +364,7 @@
             def _():
                 rows[rs, cols(k)] = picked
 
-        row_swap.append(swap(rows_out.at[rs, 0:direct], rows.at[rs, 0:direct]))
+        row_swap.append(swap(rows_out.at[rs, 0:direct], rows.at[rs, 0:direct], row_sent))
         send(row_swap[-1])
     @pl.when(leads)
     def _():
@@ -348,9 +385,9 @@
             for copy in pool_out:
                 copy.start()
     spread_moved(0, 1, 2)
-    forward(0, 0)
-    for load in loads[4:]:
-        load.wait()
+    forward(0)
+    for copy in loads[3:6]:
+        copy.wait()
     turned(edge.at[2], 1)
 
     def differences(m, at):
@@ -366,12 +403,12 @@
     @pl.when(moves)
     def _():
         choose(jnp.broadcast_to(lab_in[1][0:1, :], (LANES, batch)).T)
-        for copy in pool_out:
-            copy.wait_recv()
+        landed(others, pool_landed)
     @pl.when(moves)
     def _():
         for k in range(direct // TILE, tiles):
             rows[:, cols(k)] = picked_of(everyone, pool_x, cols(k - direct // TILE))
+    forward(1)
     gathered(0)
 
     def activate(rs):
@@ -391,30 +428,39 @@
             resid[rs, at] = value
             resid_t[at, rs] = value.T
 
-    ups = [remote(near.at[m], before.at[m], (lax.rem(ci + 1, c), me)) for m in range(3)]
-    downs = [remote(near.at[m], after.at[m], (lax.rem(ci + c - 1, c), me)) for m in range(3)]
+    ups = remote(near, before, (lax.rem(ci + 1, c), me))
+    downs = remote(near, after, (lax.rem(ci + c - 1, c), me))
     has_next, has_prev = ci < c - 1, ci > 0
 
     for b, rs in enumerate(blocks):
+        if b == len(blocks) - 1:
+
+            @pl.when(moves)
+            def _():
+                for key in parts[:-1]:
+                    forward(key)
         arrive(row_swap[b])
         activate(rs)
         if b == 0:
-            forward(1, 1)
+            @pl.when(leads)
+            def _():
+                for key in parts:
+                    forward(key)
             gathered(1)
             @pl.when(has_next)
             def _():
-                for copy in ups:
-                    copy.start()
+                ups.start()
 
             @pl.when(has_prev)
             def _():
-                for copy in downs:
-                    copy.start()
+                downs.start()
 
         if b == len(blocks) - 1:
-            forward(2, 2)
+
+            @pl.when(moves)
+            def _():
+                forward(parts[-1])
         residual(rs)
-    gathered(2)
 
     def classify(t, energy):
         at = column(t)
@@ -436,21 +482,30 @@
             of = pl.ds(pl.multiple_of(r * half, half), half)
             grad[m, of, at] = dot_nn(left_t[of, :], right[:, at]).astype(BF16)
 
-    to_core, to_pair, to_home = {}, {}, {}
+    to_pair, to_home, core_in, pair_in = {}, {}, {}, {}
+    core_sent, home_sent = ticket(0), ticket(0)
+    pair_sent = [ticket(0) for _ in range(1, pairs)]
 
     def scatter(key, m, at):
-        to_core[key] = [
-            begin(remote(piece(grad, m, 2 * q + 1 - core, at), from_core.at[m, q, :, at], twin))
-            for q in range(pairs)
-        ]
+        core_in[key], pair_in[key] = ticket(1), ticket(1)
+        for q in range(pairs):
+            remote(
+                piece(grad, m, 2 * q + 1 - core, at),
+                from_core.at[m, q, :, at],
+                twin,
+                core_sent,
+                core_in[key],
+            ).start()
         to_pair[key] = []
         for d in range(1, pairs):
             q = pair_at(d)
             held = piece(grad, m, 2 * q + core, at)
-            to_pair[key].append(remote(held, from_pair.at[m, d - 1, :, at], (ci, 2 * q + side)))
-        started.extend(to_pair[key])
+            into = from_pair.at[m, d - 1, :, at]
+            to_pair[key].append(
+                remote(held, into, (ci, 2 * q + side), pair_sent[d - 1], pair_in[key])
+            )
         held = piece(grad, m, 2 * pair + core, at)
-        to_home[key] = swap(held, last.at[m, :, at])
+        to_home[key] = swap(held, last.at[m, :, at], home_sent)
 
     def combine(m, into, index, terms, at):
         @pl.loop(0, block // step)
@@ -463,8 +518,7 @@
             into[pl.ds(off, step), :] = total.astype(BF16)
 
     def scatter_on(key, m, at):
-        for copy in to_core[key]:
-            copy.wait_recv()
+        landed(from_core.at[m, :, :, at], core_in[key])
         for d in range(1, pairs):
             q = pair_at(d)
             held = piece(grad, m, 2 * q + core, at)
@@ -472,8 +526,8 @@
             to_pair[key][d - 1].start()
 
     def scatter_home(key, m, at):
-        for copy in to_pair[key]:
-            copy.wait_recv()
+        if pairs > 1:
+            landed(from_pair.at[m, :, :, at], pair_in[key])
         terms = [from_core.at[m, pair, :, at]]
         terms += [from_pair.at[m, d, :, at] for d in range(pairs - 1)]
 
@@ -498,11 +552,14 @@
 
     energy = zero
     for t in range(tiles):
+        gathered(parts[t])
         energy = classify(t, energy)
+        if t > 0:
+            moved_on((2, t - 1), 2, cols(t - 1))
+        if t == tiles - 1 and tiles > 1:
+            led_on((2, 0), 2, cols(0))
         product(2, resid_t, dlog, cols(t))
         scatter((2, t), 2, cols(t))
-        if t > 0:
-            moved_on((2, t - 1), 2, cols(t - 1))
 
     power[0] = energy * (0.5 * norm)
     power_swap = swap(power.at[0], power.at[1])
@@ -513,20 +570,19 @@
         dres[:, at] = dot_nt(dlog[...], wide[2, at, :]).astype(BF16)
         if t == 0:
             moved_on((2, tiles - 1), 2, cols(tiles - 1))
-        led_on((2, t), 2, at)
+        if t > 0 or tiles == 1:
+            led_on((2, t), 2, at)
         product(1, hid_t, dres, at)
         scatter((1, t), 1, at)
         if t > 0:
             scatter_on((1, t - 1), 1, cols(t - 1))
     @pl.when(has_prev)
     def _():
-        for copy in ups:
-            copy.wait_recv()
+        ups.wait_recv()
 
     @pl.when(has_next)
     def _():
-        for copy in downs:
-            copy.wait_recv()
+        downs.wait_recv()
 
     def span_sums(m, carry):
         def body(r, carry):
@@ -544,27 +600,31 @@
         carry = span_sums(m, carry)
     for k in range(3):
         sums[me, k] = carry[k]
-    sums_out = [
-        begin(remote(sums.at[me], sums.at[me], (ci, lax.rem(me + d, n)))) for d in range(1, n)
-    ]
+    sums_sent, sums_landed = ticket(0), ticket(1)
+    for d in range(1, n):
+        remote(
+            sums.at[me], sums.at[me], (ci, lax.rem(me + d, n)), sums_sent, sums_landed
+        ).start()
     @pl.loop(0, tiles)
     def _(t):
         at = column(t)
         rows_t[at, :] = rows[:, at].T
     scatter_on((1, tiles - 1), 1, cols(tiles - 1))
 
-    for t in range(tiles):
-        at = cols(t)
+    ends = [cols(t) for t in range(tiles - 1)]
+    ends += [pl.ds(width - 2 * LANES, LANES), pl.ds(width - LANES, LANES)]
+    for t, at in enumerate(ends):
         dlog[:, at] = (dot_nt(dres[...], wide[1, at, :]) * slope[:, at]).astype(BF16)
         product(0, rows_t, dlog, at)
         scatter((0, t), 0, at)
         if t > 0:
-            scatter_on((0, t - 1), 0, cols(t - 1))
-
-        @pl.when(moves)
-        def _():
-            scatter_home((2, t), 2, at)
-    scatter_on((0, tiles - 1), 0, cols(tiles - 1))
+            scatter_on((0, t - 1), 0, ends[t - 1])
+        if t < tiles:
+
+            @pl.when(moves)
+            def _():
+                scatter_home((2, t), 2, cols(t))
+    scatter_on((0, tiles), 0, ends[tiles])
 
     @pl.when(leads)
     def _():
@@ -585,8 +645,7 @@
     carry = (zero, zero)
     for t in range(tiles):
         scatter_home((1, t), 1, cols(t))
-    for copy in sums_out:
-        copy.wait_recv()
+    landed(sums.at[pl.ds(0, n - 1)], sums_landed)
 
     def over_dp(ref, k):
         total = ref[0, k]
@@ -605,9 +664,11 @@
     raw_len = jnp.sqrt(raw_sq + EPS)
     spans[ci, 0] = jnp.broadcast_to(len_behind, (8, LANES))
     spans[ci, 1] = jnp.broadcast_to(len_ahead, (8, LANES))
-    spans_out = [
-        begin(remote(spans.at[ci], spans.at[ci], (lax.rem(ci + d, c), me))) for d in range(1, c)
-    ]
+    spans_sent, spans_landed = ticket(0), ticket(1)
+    for d in range(1, c):
+        remote(
+            spans.at[ci], spans.at[ci], (lax.rem(ci + d, c), me), spans_sent, spans_landed
+        ).start()
     by_ahead = 1.0 / (len_ahead * raw_len)
     by_behind = 1.0 / (len_behind * raw_len)
     for m in range(3):
@@ -620,21 +681,39 @@
 
         lax.fori_loop(0, block // step, body, 0)
 
+    def flipped(source, cs, store):
+        for low in range(0, block, LANES):
+            at = pl.ds(low, min(LANES, block - low))
+            for k in range(cs.start // LANES, (cs.start + cs.size) // LANES):
+                top = min(classes - k * LANES, LANES)
+                store(k * LANES, top, at, source[at, k * LANES : (k + 1) * LANES].T)
+
+    def keep_tau(low, top, at, value):
+        o_out[0, low : low + top, at] = value[0:top, :]
+
+    def keep_grad(low, top, at, value):
+        thin[1, low : low + top, at] = value[0:top, :]
+
+    flipped(tau_out, everything, keep_tau)
     for i in range(tiles):
         carry = finish((2, i), 2, cols(i), carry)
-        scatter_home((0, i), 0, cols(i))
-    for m in (1, 0):
-        for t in range(tiles):
-            carry = finish((m, t), m, cols(t), carry)
+        flipped(edge.at[2], cols(i), keep_grad)
+        scatter_home((0, i), 0, ends[i])
+    scatter_home((0, tiles), 0, ends[tiles])
+    for t in range(tiles):
+        carry = finish((1, t), 1, cols(t), carry)
+    for t, at in enumerate(ends):
+        carry = finish((0, t), 0, at, carry)
     arrive(power_swap)
     late[me, 0] = carry[0]
     late[me, 1] = carry[1]
     late[me, 2] = jnp.where(leads, power[0], power[1])
-    late_out = [
-        begin(remote(late.at[me], late.at[me], (ci, lax.rem(me + d, n)))) for d in range(1, n)
-    ]
-    for copy in spans_out:
-        copy.wait_recv()
+    late_sent, late_landed = ticket(0), ticket(1)
+    for d in range(1, n):
+        remote(
+            late.at[me], late.at[me], (ci, lax.rem(me + d, n)), late_sent, late_landed
+        ).start()
+    landed(spans.at[pl.ds(0, c - 1)], spans_landed)
     arc = jnp.zeros((1, 1), F32)
     band = jnp.zeros((1, 1), F32)
     for k in range(c):
@@ -642,8 +721,7 @@
         arc = arc + jnp.where(k <= ci, length, 0.0)
         band = band + length
     band = band + spans[c - 1, 1, 0:1, 0:1]
-    for copy in late_out:
-        copy.wait_recv()
+    landed(late.at[pl.ds(0, n - 1)], late_landed)
     along, g_g, energy_all = (over_dp(late, k) for k in range(3))
 
     goal = (ci + 1).astype(F32) / (c + 1) * band
@@ -658,18 +736,10 @@
     o_small[0:1, :] = small(energy_all)
     o_small[1:2, :] = small(arc / band)
     o_small[2:3, :] = small(0.5 * raw_len)
-    @pl.loop(0, classes // LANES)
-    def _(k):
-        at = pl.ds(pl.multiple_of(k * LANES, LANES), LANES)
-        new = own[2, :, at] + (push * tau_out[:, at] - scale * edge[2, :, at])
-        o_out[0, at, :] = new.T
-
-    rest = classes % LANES
-    if rest:
-        low = classes - rest
-        at = pl.ds(low, LANES)
-        new = own[2, :, at] + (push * tau_out[:, at] - scale * edge[2, :, at])
-        o_out[0, low:classes, :] = new.T[0:rest, :]
+    for low in range(0, classes, LANES):
+        at = pl.ds(low, min(LANES, classes - low))
+        o_out[0, at, :] = thin[0, at, :] + (push * o_out[0, at, :] - scale * thin[1, at, :])
+
     for m in range(2):
 
         @pl.loop(0, block // step)
@@ -678,21 +748,29 @@
             tau[m][at, :] = own[m, at, :] + (push * tau[m][at, :] - scale * edge[m, at, :])
     @pl.when(has_next)
     def _():
-        for copy in ups:
+        ups.wait_send()
+
+    @pl.when(has_prev)
+    def _():
+        downs.wait_send()
+
+    @pl.when(moves)
+    def _():
+        sent(stage, hop_out)
+        sent(rows_out.at[:, 0:direct], row_sent)
+        sent(others, pool_sent)
+        sent(last, home_sent)
+        for copy in (pool_swap, lab_swap, power_swap):
             copy.wait_send()
 
-    @pl.when(has_prev)
-    def _():
-        for copy in downs:
-            copy.wait_send()
-
-    @pl.when(moves)
-    def _():
-        for copy in swapped + pool_out:
-            copy.wait_send()
-
-    for copy in started:
-        copy.wait_send()
+    for out in across_out + over_out:
+        sent(stage, out)
+    sent(from_core, core_sent)
+    for out in pair_sent:
+        sent(last, out)
+    sent(sums.at[pl.ds(0, n - 1)], sums_sent)
+    sent(spans.at[pl.ds(0, c - 1)], spans_sent)
+    sent(late.at[pl.ds(0, n - 1)], late_sent)
 
 
 def on_device(
@@ -714,7 +792,7 @@
     depth = n * block
     batch = batch_rows.shape[1]
     pairs = n // 2
-    copies = copies_of(n, c, width // TILE, 3)
+    sends, receives = semaphores(n, width // TILE, 3)
     vmem = pl.BlockSpec(memory_space=pltpu.VMEM)
     anywhere = pl.BlockSpec(memory_space=pl.ANY)
     scalar = pl.BlockSpec(memory_space=pltpu.SMEM)
@@ -761,9 +839,9 @@
             pltpu.VMEM((n, 3, 8, LANES), F32),
             pltpu.VMEM((c, 2, 8, LANES), F32),
             pltpu.VMEM((n, 3, 8, LANES), F32),
-            pltpu.SemaphoreType.DMA((7,)),
-            pltpu.SemaphoreType.DMA((copies,)),
-            pltpu.SemaphoreType.DMA((copies,)),
+            pltpu.SemaphoreType.DMA((6 + c // 2,)),
+            pltpu.SemaphoreType.DMA((sends,)),
+            pltpu.SemaphoreType.DMA((receives,)),
         ],
         compiler_params=pltpu.CompilerParams(
             collective_id=0, has_side_effects=True, vmem_limit_bytes=60 * 1024 * 1024

time: 95.7 us -> 92.6 us (0.968)
  Pallas kernels: 90.8 us -> 87.7 us
    pallas_call x1, Pallas kernels: 90.8 us -> 87.7 us  [on_device(): pl.pallas_call(functools.partial(kernel, n, c, classes), out_shape=(pltpu...]
where the time goes in v4:
time: 92.6 us; the launch traced here: 92.4 us
  Pallas kernels  87.7 us (95%)
  local copies, waits for them, and re-layouts  3.42 us (4%)
  between operations  1.29 us (1%)
    pallas_call x1, Pallas kernels, on_device(): pl.pallas_call(functools.partial(kernel, n, c, classes), out_shape=(pltpu...  87.7 us
    unnamed x3, local copies, waits for them, and re-layouts  2.9 us

profile of v4, /device:TPU:0, one launch (start us, length us, event | category | flops | bytes accessed | tf_op | source)
XLA Modules:
  0.0 92.4 jit_solution(15748857156350732613)
XLA Ops:
  1.3 87.7 %shard_map.145 = (f32[1,256,1024]{2,1,0:T(8,128)S(1)}, f32[1,256,1024]{2,1,0:T(8,128)S(1)}, f32[1,1000,256]{2,1,0:T(8,128)S(1)}, f32[8,128]{1,0:T(8,128)S(1)}) custom-call(f32[1,256,1024]{2,1,0:T(8,128)} %p_in.1, f32[1,256,1024]{2,1,0:T(8,128)} %p_mid.1, f32[1,1000,256]{2,1,0:T(8,128)} %bitcast.8, f32[2,256,1024]{2,1,0:T(8,128)} %e_in.1, ...), custom_call_target="tpu_custom_call" | custom-call | tf_op jit(solution)/shard_map/pallas_call | solution.py:799
  89.0 0.5 fusion
  89.5 1.0 %copy.19 = f32[1,256,1024]{2,1,0:T(8,128)} copy(f32[1,256,1024]{2,1,0:T(8,128)S(1)} %get-tuple-element.17) | data formatting | bytes 2097152
  90.5 1.0 %copy.20 = f32[1,256,1024]{2,1,0:T(8,128)} copy(f32[1,256,1024]{2,1,0:T(8,128)S(1)} %get-tuple-element.18) | data formatting | bytes 2097152
  91.4 1.0 %copy.21 = f32[1,256,1000]{1,2,0:T(8,128)} copy(f32[1,256,1000]{1,2,0:T(8,128)S(1)} %bitcast.6) | data formatting | bytes 2048000

commit v5 on v4

--- a/solution.py
+++ b/solution.py
@@ -57,8 +57,8 @@
     e_mid,
     e_out,
     pool,
-    picks,
-    labs,
+    picks_h,
+    labs_h,
     climb,
     o_in,
     o_mid,
@@ -75,6 +75,7 @@
     after,
     pool_v,
     pool_x,
+    both,
     lab_t,
     lab_out,
     lab_in,
@@ -170,12 +171,14 @@
         load(3, e_in.at[end], edge.at[0]),
         load(4, e_mid.at[end], edge.at[1]),
         load(5, e_out.at[end], thin.at[1, pl.ds(0, classes)]),
+        load(6, picks_h, both.at[1, 0:1]),
+        load(7, labs_h, both.at[0, 0:1]),
     ]
     pool_loads = [
-        load(6 + d, pool.at[pool_rows(d)], pool_v.at[pool_rows(d)]) for d in range(planes)
+        load(8 + d, pool.at[pool_rows(d)], pool_v.at[pool_rows(d)]) for d in range(planes)
     ]
     for copy in (
-        [pool_loads[0], loads[0]] + loads[1:3] + pool_loads[1:] + loads[3:6]
+        [pool_loads[0], loads[0]] + loads[6:8] + loads[1:3] + pool_loads[1:] + loads[3:6]
     ):
         copy.start()
 
@@ -211,7 +214,7 @@
         return pl.ds(pl.multiple_of(t * TILE, TILE), TILE)
 
     everything, everyone = pl.ds(0, width), pl.ds(0, batch)
-    cuts = [0] + [at for at in (batch - 4 * LANES, batch - LANES) if at > 0] + [batch]
+    cuts = [0] + [at for at in (batch - 3 * LANES, batch - LANES) if at > 0] + [batch]
     blocks = [pl.ds(low, high - low) for low, high in zip(cuts[:-1], cuts[1:])]
 
     def piece(ref, m, index, at=everything):
@@ -325,8 +328,10 @@
     lowered(2)
     send(hop[2])
     spread_own(*parts)
-    lab_out[0] = jnp.broadcast_to(labs[...], (8, batch))
-    lab_out[1] = jnp.broadcast_to(picks[...], (8, batch))
+    loads[6].wait()
+    loads[7].wait()
+    lab_out[0] = jnp.broadcast_to(both[0][0:1, :], (8, batch))
+    lab_out[1] = jnp.broadcast_to(both[1][0:1, :], (8, batch))
 
     @pl.when(leads)
     def _():
@@ -350,7 +355,7 @@
             dot_nn(grad[m, rs, 0:size], source[pl.ds(m * width, size), at]) for m, size in reach
         ).astype(BF16)
 
-    choose(jnp.broadcast_to(picks[...], (LANES, batch)).T)
+    choose(jnp.broadcast_to(both[1][0:1, :], (LANES, batch)).T)
     for copy in pool_loads[1:]:
         copy.wait()
     direct = width - pool_x.shape[1]
@@ -618,13 +623,13 @@
         product(0, rows_t, dlog, at)
         scatter((0, t), 0, at)
         if t > 0:
-            scatter_on((0, t - 1), 0, ends[t - 1])
+            moved_on((0, t - 1), 0, ends[t - 1])
         if t < tiles:
 
             @pl.when(moves)
             def _():
                 scatter_home((2, t), 2, cols(t))
-    scatter_on((0, tiles), 0, ends[tiles])
+    moved_on((0, tiles), 0, ends[tiles])
 
     @pl.when(leads)
     def _():
@@ -645,6 +650,9 @@
     carry = (zero, zero)
     for t in range(tiles):
         scatter_home((1, t), 1, cols(t))
+        if t == tiles // 2:
+            for k, at in enumerate(ends):
+                led_on((0, k), 0, at)
     landed(sums.at[pl.ds(0, n - 1)], sums_landed)
 
     def over_dp(ref, k):
@@ -699,15 +707,16 @@
         carry = finish((2, i), 2, cols(i), carry)
         flipped(edge.at[2], cols(i), keep_grad)
         scatter_home((0, i), 0, ends[i])
-    scatter_home((0, tiles), 0, ends[tiles])
     for t in range(tiles):
         carry = finish((1, t), 1, cols(t), carry)
+    scatter_home((0, tiles), 0, ends[tiles])
     for t, at in enumerate(ends):
         carry = finish((0, t), 0, at, carry)
     arrive(power_swap)
-    late[me, 0] = carry[0]
-    late[me, 1] = carry[1]
-    late[me, 2] = jnp.where(leads, power[0], power[1])
+    terms = (carry[0], carry[1], jnp.where(leads, power[0], power[1]))
+    for k, term in enumerate(terms):
+        late[me, k : k + 1, :] = jnp.sum(term, axis=0, keepdims=True)
+    late[me, 3:8, :] = jnp.zeros((5, LANES), F32)
     late_sent, late_landed = ticket(0), ticket(1)
     for d in range(1, n):
         remote(
@@ -722,7 +731,11 @@
         band = band + length
     band = band + spans[c - 1, 1, 0:1, 0:1]
     landed(late.at[pl.ds(0, n - 1)], late_landed)
-    along, g_g, energy_all = (over_dp(late, k) for k in range(3))
+    closing = late[0]
+    for j in range(1, n):
+        closing = closing + late[j]
+    closing = jnp.sum(closing, axis=1, keepdims=True)
+    along, g_g, energy_all = closing[0:1], closing[1:2], closing[2:3]
 
     goal = (ci + 1).astype(F32) / (c + 1) * band
     coef = jnp.where(jnp.full((1, 1), climb[0]) == 1, 2.0 * along, along + SPRING * (goal - arc) / band)
@@ -804,7 +817,7 @@
             pltpu.VMEM((1, classes, block), F32),
             pltpu.VMEM((8, LANES), F32),
         ),
-        in_specs=[anywhere] * 7 + [vmem] * 2 + [scalar],
+        in_specs=[anywhere] * 9 + [scalar],
         out_specs=[vmem] * 4,
         scratch_shapes=[
             pltpu.VMEM((3, block, width), F32),
@@ -818,6 +831,7 @@
             pltpu.VMEM((3, block, width), BF16),
             pltpu.VMEM(data_pool.shape, BF16),
             pltpu.VMEM((data_pool.shape[0], width // 2), BF16),
+            pltpu.VMEM((2, 8, batch), jnp.int32),
             pltpu.VMEM((batch, LANES), jnp.int32),
             pltpu.VMEM((2, 8, batch), jnp.int32),
             pltpu.VMEM((2, 8, batch), jnp.int32),
@@ -838,8 +852,8 @@
             pltpu.VMEM((2, 8, LANES), F32),
             pltpu.VMEM((n, 3, 8, LANES), F32),
             pltpu.VMEM((c, 2, 8, LANES), F32),
-            pltpu.VMEM((n, 3, 8, LANES), F32),
-            pltpu.SemaphoreType.DMA((6 + c // 2,)),
+            pltpu.VMEM((n, 8, LANES), F32),
+            pltpu.SemaphoreType.DMA((8 + c // 2,)),
             pltpu.SemaphoreType.DMA((sends,)),
             pltpu.SemaphoreType.DMA((receives,)),
         ],

time: 92.6 us -> 91.5 us (0.988)
  Pallas kernels: 87.7 us -> 86.7 us
    pallas_call x1, Pallas kernels: 87.7 us -> 86.7 us  [on_device(): pl.pallas_call(functools.partial(kernel, n, c, classes), out_shape=(pltpu...]
where the time goes in v5:
time: 91.5 us; the launch traced here: 91.4 us
  Pallas kernels  86.7 us (95%)
  local copies, waits for them, and re-layouts  3.42 us (4%)
  between operations  1.29 us (1%)
    pallas_call x1, Pallas kernels, on_device(): pl.pallas_call(functools.partial(kernel, n, c, classes), out_shape=(pltpu...  86.7 us
    unnamed x3, local copies, waits for them, and re-layouts  2.9 us

profile of v5, /device:TPU:0, one launch (start us, length us, event | category | flops | bytes accessed | tf_op | source)
XLA Modules:
  0.0 91.4 jit_solution(16455323846879749919)
XLA Ops:
  1.3 86.7 %shard_map.145 = (f32[1,256,1024]{2,1,0:T(8,128)S(1)}, f32[1,256,1024]{2,1,0:T(8,128)S(1)}, f32[1,1000,256]{2,1,0:T(8,128)S(1)}, f32[8,128]{1,0:T(8,128)S(1)}) custom-call(f32[1,256,1024]{2,1,0:T(8,128)} %p_in.1, f32[1,256,1024]{2,1,0:T(8,128)} %p_mid.1, f32[1,1000,256]{2,1,0:T(8,128)} %bitcast.8, f32[2,256,1024]{2,1,0:T(8,128)} %e_in.1, ...), custom_call_target="tpu_custom_call" | custom-call | tf_op jit(solution)/shard_map/pallas_call | solution.py:812
  88.0 0.5 fusion
  88.5 1.0 %copy.19 = f32[1,256,1024]{2,1,0:T(8,128)} copy(f32[1,256,1024]{2,1,0:T(8,128)S(1)} %get-tuple-element.17) | data formatting | bytes 2097152
  89.5 1.0 %copy.20 = f32[1,256,1024]{2,1,0:T(8,128)} copy(f32[1,256,1024]{2,1,0:T(8,128)S(1)} %get-tuple-element.18) | data formatting | bytes 2097152
  90.4 1.0 %copy.21 = f32[1,256,1000]{1,2,0:T(8,128)} copy(f32[1,256,1000]{1,2,0:T(8,128)S(1)} %bitcast.6) | data formatting | bytes 2048000

commit v6 on v5

--- a/solution.py
+++ b/solution.py
@@ -650,7 +650,7 @@
     carry = (zero, zero)
     for t in range(tiles):
         scatter_home((1, t), 1, cols(t))
-        if t == tiles // 2:
+        if t == tiles - 1:
             for k, at in enumerate(ends):
                 led_on((0, k), 0, at)
     landed(sums.at[pl.ds(0, n - 1)], sums_landed)

time: 91.5 us -> 91.6 us (level)
  no operation moved by 1% of the time
where the time goes in v6:
time: 91.6 us; the launch traced here: 91.4 us
  Pallas kernels  86.7 us (95%)
  local copies, waits for them, and re-layouts  3.42 us (4%)
  between operations  1.29 us (1%)
    pallas_call x1, Pallas kernels, on_device(): pl.pallas_call(functools.partial(kernel, n, c, classes), out_shape=(pltpu...  86.7 us
    unnamed x3, local copies, waits for them, and re-layouts  2.9 us

profile of v6, /device:TPU:0, one launch (start us, length us, event | category | flops | bytes accessed | tf_op | source)
XLA Modules:
  0.0 91.4 jit_solution(17927642071724543452)
XLA Ops:
  1.3 86.7 %shard_map.145 = (f32[1,256,1024]{2,1,0:T(8,128)S(1)}, f32[1,256,1024]{2,1,0:T(8,128)S(1)}, f32[1,1000,256]{2,1,0:T(8,128)S(1)}, f32[8,128]{1,0:T(8,128)S(1)}) custom-call(f32[1,256,1024]{2,1,0:T(8,128)} %p_in.1, f32[1,256,1024]{2,1,0:T(8,128)} %p_mid.1, f32[1,1000,256]{2,1,0:T(8,128)} %bitcast.8, f32[2,256,1024]{2,1,0:T(8,128)} %e_in.1, ...), custom_call_target="tpu_custom_call" | custom-call | tf_op jit(solution)/shard_map/pallas_call | solution.py:812
  88.0 0.5 fusion
  88.5 1.0 %copy.19 = f32[1,256,1024]{2,1,0:T(8,128)} copy(f32[1,256,1024]{2,1,0:T(8,128)S(1)} %get-tuple-element.17) | data formatting | bytes 2097152
  89.5 1.0 %copy.20 = f32[1,256,1024]{2,1,0:T(8,128)} copy(f32[1,256,1024]{2,1,0:T(8,128)S(1)} %get-tuple-element.18) | data formatting | bytes 2097152
  90.5 1.0 %copy.21 = f32[1,256,1000]{1,2,0:T(8,128)} copy(f32[1,256,1000]{1,2,0:T(8,128)S(1)} %bitcast.6) | data formatting | bytes 2048000
